TPU v7x, 32 devices: a whole 2x2x4 slice. The times are simulated.
32 devices in a mesh: grp: 2 (over x), gx: 8 (over z, y), gy: 2 (over core).
Axes of the slice: x: 2, y: 2, z: 4, core: 2. Of those that a mesh axis runs over, the one named last changes fastest.
Arguments:
- warmth_anomaly: float32 [64, 128, 256], P('grp', 'gx', 'gy'), may hold values from -6 to 6
- humidity_anomaly: float32 [64, 128, 256], P('grp', 'gx', 'gy'), may hold values from -6 to 6
- horizontal_line_advective_ratio: float32 [64], replicated, may hold values from -0.5 to 0.5
- vertical_line_advective_ratio: float32 [64], replicated, may hold values from -0.5 to 0.5
- molecular_extinction_coefficient: float32 [112], replicated, may hold values from 0.002 to 0.05
- droplet_extinction_thickness: float32 [112], replicated, may hold values from 0.005 to 0.1
- shortwave_quadrature_share: float32 [112], replicated, may hold values from 0.5 to 5
- longwave_quadrature_share: float32 [112], replicated, may hold values from 0.5 to 5
- overcast_layer_flags: int32 [8192, 64], P(('grp', 'gx', 'gy')), may hold values 0 or 1
- profile_position_within_tile: int32 [64, 128], P('gx', 'gy'), may hold values from 0 to 511, as said below
Outputs:
- temperature_out: float32 [64, 128, 256], P('grp', 'gx', 'gy')
- moisture_out: float32 [64, 128, 256], P('grp', 'gx', 'gy')
- warming_rates: float32 [8192, 64], P(('grp', 'gx', 'gy'))
Inputs may be any that keep to these rules, and one draw needn't show every extreme that they name: `profile_position_within_tile`: each tile's block of 8 x 64 entries holds every number from 0 to 511 exactly once.
All inputs are finite; a program needn't handle non-finite values. No bound on the sum of `overcast_layer_flags` on one device may be relied on, other than what follows from the above.
Results may differ from a plain program's by a relative error of at most 0.000092.
Values sent between devices are 32-bit elements; how exact they have to be, the bound alone decides.
A program may use at most 64 MiB of HBM per device.

v0:
```python
import functools
import math

import jax
import jax.numpy as jnp
from jax import lax
from jax.experimental import pallas as pl
from jax.experimental.pallas import tpu as pltpu
from jax.sharding import PartitionSpec as P

SWEEPS = 8
NU_H = 0.15
NU_V = 0.15
HEATING_INTERVAL = 0.5
UNROLL = 8
M = 8
MESH = pl.DeviceIdType.MESH
BF = jnp.bfloat16
F32 = jnp.float32


def split_bf16(x):
    hi = x.astype(BF)
    lo = (x - hi.astype(F32)).astype(BF)
    return hi, lo


def kernel(
    n_gx, n_gy, L, R, C, S, B, G,
    warm_in, humid_in, cx_ref, cy_ref, gas_ref, drop_ref, sw_ref, lw_ref, flags_ref, slot_ref,
    t_out, m_out, rates_out,
    ext0, ext1, edge_send, edge_recv, qt, packed, rad, coef, cloudy, absorber, theta, rates, heat, ucols,
    hedge_send, hedge_recv, rows_send, rows_recv,
    halo_send_sem, halo_recv_sem, edge_send_sem, edge_recv_sem, misc_send_sem, misc_recv_sem,
):
    g = lax.axis_index("grp")
    x = lax.axis_index("gx")
    y = lax.axis_index("gy")
    og = 1 - g
    xn, xp = lax.rem(x + 1, n_gx), lax.rem(x + n_gx - 1, n_gx)
    yn, yp = lax.rem(y + 1, n_gy), lax.rem(y + n_gy - 1, n_gy)
    fields = (warm_in, humid_in)
    ext = (ext0, ext1)
    outs = (t_out, m_out)
    LE = L + M
    T = (R + 2 * M) // 8
    per = C // T
    NP = -(-LE // per)
    RI = R // 2
    RLO = 8
    ROWN = RLO + M
    RE = R + 2 * M

    barrier = pltpu.get_barrier_semaphore()
    for dev in ((g, xn, y), (g, xp, y), (og, x, y), (og, xn, y), (og, xp, y), (g, x, yn), (g, x, yp)):
        pl.semaphore_signal(barrier, inc=1, device_id=dev, device_id_type=MESH)
    pl.semaphore_wait(barrier, 7)

    def remote(src, dst, ss, rs, dev):
        c = pltpu.make_async_remote_copy(
            src_ref=src, dst_ref=dst, send_sem=ss, recv_sem=rs, device_id=dev, device_id_type=MESH
        )
        c.start()
        return c

    half = slot_ref.shape[1]
    slots = slot_ref[...]
    rep = (
        lax.broadcasted_iota(jnp.int32, (half, C), 1) // 2
        == lax.broadcasted_iota(jnp.int32, (half, C), 0)
    ).astype(F32).astype(BF)
    s_hi = (slots // 16).astype(F32).astype(BF)
    s_lo = (slots % 16).astype(F32).astype(BF)
    slot_rep = (
        16.0 * jnp.dot(s_hi, rep, preferred_element_type=F32)
        + jnp.dot(s_lo, rep, preferred_element_type=F32)
    ).astype(jnp.int32)
    s_iota = lax.broadcasted_iota(jnp.int32, (S, C), 0)
    for i in range(RI):
        qt[:, i * C : (i + 1) * C] = jnp.where(s_iota == slot_rep[i : i + 1, :], 1.0, 0.0).astype(BF)
    parts = []
    for i in range(RI):
        col = []
        for f in range(2):
            flat = fields[f].reshape(L * R, C)
            col.append(
                flat[pl.ds(2 * i, L, stride=R), :] + flat[pl.ds(2 * i + 1, L, stride=R), :]
            )
        hi, lo = split_bf16(0.25 * jnp.concatenate(col, axis=0))
        parts.append(jnp.concatenate([hi, lo], axis=0))
    lhs = jnp.concatenate(parts, axis=1)
    both = lax.dot_general(
        lhs, qt[...], (((1,), (1,)), ((), ())), preferred_element_type=F32
    )
    both = both[: 2 * L] + both[2 * L :]
    for h in range(2):
        packed[h] = both[:, h * B : (h + 1) * B]
    c_packed = remote(packed.at[og], rad.at[g], misc_send_sem.at[0], misc_recv_sem.at[0], (og, x, y))

    lev_src = (L - M) * og
    lev_dst = 1 + L * g
    own_dst = 1 + M * g
    halos = []
    n = 0
    for f in range(2):
        for levs, dlevs, count, gg in ((0, own_dst, L, g), (lev_src, lev_dst, M, og)):
            for r0, d0, xx in ((R - M, RLO, xn), (0, ROWN + R, xp)):
                halos.append(remote(
                    fields[f].at[pl.ds(levs, count), r0 : r0 + M, :],
                    ext0.at[f, pl.ds(dlevs, count), d0 : d0 + M, :],
                    halo_send_sem.at[n], halo_recv_sem.at[n], (gg, xx, y),
                ))
                n += 1
        halos.append(remote(
            fields[f].at[pl.ds(lev_src, M)],
            ext0.at[f, pl.ds(lev_dst, M), ROWN : ROWN + R, :],
            halo_send_sem.at[n], halo_recv_sem.at[n], (og, x, y),
        ))
        n += 1
    rad[g] = packed[g]
    for f in range(2):
        ext0[f, pl.ds(own_dst, L), ROWN : ROWN + R, :] = fields[f][...]
        for b in range(2):
            for p in (0, LE + 1):
                ext[b][f, p] = jnp.zeros((RE + 16, C), F32)

    log2e = 1.0 / math.log(2.0)
    for q, (ref, scale) in enumerate(((gas_ref, -log2e), (drop_ref, -log2e), (sw_ref, 1.0), (lw_ref, 1.0))):
        coef[q] = jnp.broadcast_to(ref[...] * scale, (128, G)).T
    for hb in range(B // 128):
        cloudy[hb] = flags_ref[:, hb * 128 : (hb + 1) * 128].astype(F32)

    c_packed.wait()
    for o in range(2):
        mo = rad[o, L : 2 * L, :]
        soft = jnp.maximum(mo, 0.0) + jnp.log1p(jnp.exp(-jnp.abs(mo)))
        for hb in range(B // 128):
            absorber[hb, o * L : (o + 1) * L, :] = soft[:, hb * 128 : (hb + 1) * 128]
            theta[hb, o * L : (o + 1) * L, :] = rad[o, 0:L, hb * 128 : (hb + 1) * 128]

    GB = G // 8
    norm = 4.0 / G
    for hb in range(B // 128):
        for o in range(2):
            def level(l, flux, o=o, hb=hb):
                lg = l + o * L
                a = jnp.broadcast_to(absorber[hb, pl.ds(lg, 1), :], (8, 128))
                c = jnp.broadcast_to(cloudy[hb, pl.ds(lg, 1), :], (8, 128))
                th = 1.0 + 0.1 * theta[hb, pl.ds(lg, 1), :]
                sw = lw = None
                new = []
                for q in range(GB):
                    rows = slice(8 * q, 8 * q + 8)
                    d = 1.0 - jnp.exp2(a * coef[0, rows, :] + c * coef[1, rows, :])
                    s = flux[q] * d
                    w = coef[3, rows, :] * d
                    sw = s if sw is None else sw + s
                    lw = w if lw is None else lw + w
                    new.append(flux[q] - s)
                total = jnp.sum(sw - lw * th, axis=0, keepdims=True) * norm
                rates[o, hb, pl.ds(l, 1), :] = total
                return tuple(new)

            if o == 0:
                flux = tuple(coef[2, 8 * q : 8 * q + 8, :] for q in range(GB))
            flux = lax.fori_loop(0, L, level, flux, unroll=2)
    c_heat = remote(rates.at[og], heat.at[g], misc_send_sem.at[1], misc_recv_sem.at[1], (og, x, y))
    heat[g] = rates[g]
    for o in range(2):
        for hb in range(B // 128):
            rates_out[o * L : (o + 1) * L, hb * 128 : (hb + 1) * 128] = rates[o, hb]

    lane = lax.broadcasted_iota(jnp.int32, (8, C), 1)

    def pack(vals, j, accs):
        right, left = accs
        for t in range(T):
            k = j * T + t
            turned = pltpu.roll(vals[8 * t : 8 * t + 8, :], lax.rem(k + 1, C), 1)
            right = jnp.where(lane == k, turned, right)
            left = jnp.where(lane == lax.rem(k + 1, C), turned, left)
        return right, left

    def send_edges(k, f):
        return (
            remote(edge_send.at[k, f, 0], edge_recv.at[k, f, 0],
                   edge_send_sem.at[k, f, 0], edge_recv_sem.at[k, f, 0], (g, x, yn)),
            remote(edge_send.at[k, f, 1], edge_recv.at[k, f, 1],
                   edge_send_sem.at[k, f, 1], edge_recv_sem.at[k, f, 1], (g, x, yp)),
        )

    zero = jnp.zeros((8, C), F32)

    def run_levels(k, f, count, values):
        for p in range(NP):
            lo, hi = p * per, min(count, (p + 1) * per)
            if lo >= hi:
                edge_send[k, f, 0, p] = zero
                edge_send[k, f, 1, p] = zero
                continue
            right, left = lax.fori_loop(
                lo, hi, lambda j, accs, lo=lo: pack(values(j), j - lo, accs), (zero, zero),
                unroll=min(UNROLL, hi - lo),
            )
            edge_send[k, f, 0, p] = right
            edge_send[k, f, 1, p] = left

    def first(f):
        run_levels(0, f, LE, lambda j: ext0[f, j + 1, RLO : RLO + RE, :])
        return send_edges(0, f)

    def sweep(k, f):
        src, dst = (k - 1) % 2, k % 2
        start = g * k
        last = k == SWEEPS
        t0, t1 = (M // 8, M // 8 + R // 8) if last else (0, T)
        r0, r1 = RLO + 8 * t0, RLO + 8 * t1

        def values(j):
            lev = start + j
            p = lev + 1
            jj = j + g
            which = jj // per
            kk = (jj - which * per) * T
            from_left = edge_recv[k - 1, f, 0, which]
            from_right = edge_recv[k - 1, f, 1, which]
            lg = lev + (L - M) * g
            sx = 0.5 * cx_ref[lg]
            sy = 0.5 * cy_ref[lg]
            cen = ext[src][f, p, r0:r1, :]
            base = (
                (1.0 - 4.0 * NU_H - 2.0 * NU_V) * cen
                + NU_V * (ext[src][f, p + 1, r0:r1, :] + ext[src][f, p - 1, r0:r1, :])
                + (NU_H - sx) * ext[src][f, p, r0 + 1 : r1 + 1, :]
                + (NU_H + sx) * ext[src][f, p, r0 - 1 : r1 - 1, :]
            )
            res = []
            for t in range(t0, t1):
                q = 8 * (t - t0)
                v = cen[q : q + 8, :]
                kt = kk + t
                prev = jnp.where(lane == 0, pltpu.roll(from_left, lax.rem(C - kt, C), 1), pltpu.roll(v, 1, 1))
                nxt = jnp.where(
                    lane == C - 1, pltpu.roll(from_right, lax.rem(2 * C - 2 - kt, C), 1), pltpu.roll(v, C - 1, 1)
                )
                res.append(base[q : q + 8, :] + (NU_H - sy) * nxt + (NU_H + sy) * prev)
            new = jnp.concatenate(res, axis=0)
            if last:
                outs[f][j] = new
            else:
                ext[dst][f, p, RLO : RLO + RE, :] = new
            return new

        count = LE - k
        if last:
            @pl.loop(0, count, unroll=UNROLL)
            def _(j):
                values(j)
            return None
        run_levels(k, f, count, values)
        return send_edges(k, f)

    for c in halos:
        c.wait()
    flight = [first(0), first(1)]
    sent = []

    def advance(ks):
        for k in ks:
            for f in range(2):
                for c in flight[f]:
                    c.wait()
                flight[f] = sweep(k, f)

    advance((1, 2))

    c_heat.wait()
    hi, lo = split_bf16(jnp.concatenate([heat[h, hb] for h in range(2) for hb in range(B // 128)], axis=1))
    spread = jnp.dot(jnp.concatenate([hi, lo], axis=0), qt[...], preferred_element_type=F32)
    spread = spread[:L] + spread[L:]
    LT = L // 8
    ehi = zero
    elo = zero
    for i in range(RI):
        ui = spread[:, i * C : (i + 1) * C]
        ucols[i] = ui
        for t in range(LT):
            k = i * LT + t
            turned = pltpu.roll(ui[8 * t : 8 * t + 8, :], (k + 1) % C, 1)
            ehi = jnp.where(lane == k, turned, ehi)
            elo = jnp.where(lane == (k + 1) % C, turned, elo)
    hedge_send[0] = ehi
    hedge_send[1] = elo
    c_he = [
        remote(hedge_send.at[0], hedge_recv.at[0], misc_send_sem.at[2], misc_recv_sem.at[2], (g, x, yn)),
        remote(hedge_send.at[1], hedge_recv.at[1], misc_send_sem.at[3], misc_recv_sem.at[3], (g, x, yp)),
    ]
    advance((3,))
    for c in c_he:
        c.wait()
    from_left = hedge_recv[0]
    from_right = hedge_recv[1]
    even = lane % 2 == 0
    for i in range(RI):
        for t in range(LT):
            k = i * LT + t
            v = ucols[i, 8 * t : 8 * t + 8, :]
            prev = jnp.where(lane == 0, pltpu.roll(from_left, (C - k) % C, 1), pltpu.roll(v, 1, 1))
            nxt = jnp.where(lane == C - 1, pltpu.roll(from_right, (2 * C - 2 - k) % C, 1), pltpu.roll(v, C - 1, 1))
            w = 0.75 * v + 0.25 * jnp.where(even, prev, nxt)
            ucols[i, 8 * t : 8 * t + 8, :] = w
            if i == 0:
                rows_send[0, 8 * t : 8 * t + 8, :] = w
            if i == RI - 1:
                rows_send[1, 8 * t : 8 * t + 8, :] = w
    c_rows = [
        remote(rows_send.at[0], rows_recv.at[0], misc_send_sem.at[4], misc_recv_sem.at[4], (g, xp, y)),
        remote(rows_send.at[1], rows_recv.at[1], misc_send_sem.at[5], misc_recv_sem.at[5], (g, xn, y)),
    ]
    advance(range(4, SWEEPS + 1))
    for c in c_rows:
        c.wait()
    flat = t_out.reshape(L * R, C)
    for i in range(RI):
        v = ucols[i]
        above = rows_recv[1] if i == 0 else ucols[i - 1]
        below = rows_recv[0] if i == RI - 1 else ucols[i + 1]
        flat[pl.ds(2 * i, L, stride=R), :] = flat[pl.ds(2 * i, L, stride=R), :] + HEATING_INTERVAL * (0.75 * v + 0.25 * above)
        flat[pl.ds(2 * i + 1, L, stride=R), :] = flat[pl.ds(2 * i + 1, L, stride=R), :] + HEATING_INTERVAL * (0.75 * v + 0.25 * below)


def hand_on(t_in, m_in, r_in, t_out, m_out, r_out):
    t_out[...] = t_in[...]
    m_out[...] = m_in[...]
    r_out[...] = r_in[...]


def body(n_gx, n_gy, warm, humid, cx, cy, gas, drop, sw, lw, flags, slots):
    L, R, C = warm.shape
    S = slots.shape[0] * slots.shape[1]
    B = flags.shape[0]
    flags = flags.T
    G = gas.shape[0]
    LE = L + M
    T = (R + 2 * M) // 8
    NP = -(-LE // (C // T))
    vmem = pl.BlockSpec(memory_space=pltpu.VMEM)
    smem = pl.BlockSpec(memory_space=pltpu.SMEM)
    t, m, rates = pl.pallas_call(
        functools.partial(kernel, n_gx, n_gy, L, R, C, S, B, G),
        out_shape=(
            jax.ShapeDtypeStruct((L, R, C), F32),
            jax.ShapeDtypeStruct((L, R, C), F32),
            jax.ShapeDtypeStruct((2 * L, B), F32),
        ),
        in_specs=[vmem, vmem, smem, smem] + [vmem] * 6,
        out_specs=(vmem, vmem, vmem),
        scratch_shapes=[
            pltpu.VMEM((2, LE + 2, R + 2 * M + 16, C), F32),
            pltpu.VMEM((2, LE + 2, R + 2 * M + 16, C), F32),
            pltpu.VMEM((SWEEPS, 2, 2, NP, 8, C), F32),
            pltpu.VMEM((SWEEPS, 2, 2, NP, 8, C), F32),
            pltpu.VMEM((S, (R // 2) * C), BF),
            pltpu.VMEM((2, 2 * L, B), F32),
            pltpu.VMEM((2, 2 * L, B), F32),
            pltpu.VMEM((4, G, 128), F32),
            pltpu.VMEM((B // 128, 2 * L, 128), F32),
            pltpu.VMEM((B // 128, 2 * L, 128), F32),
            pltpu.VMEM((B // 128, 2 * L, 128), F32),
            pltpu.VMEM((2, B // 128, L, 128), F32),
            pltpu.VMEM((2, B // 128, L, 128), F32),
            pltpu.VMEM((R // 2, L, C), F32),
            pltpu.VMEM((2, 8, C), F32),
            pltpu.VMEM((2, 8, C), F32),
            pltpu.VMEM((2, L, C), F32),
            pltpu.VMEM((2, L, C), F32),
            pltpu.SemaphoreType.DMA((10,)),
            pltpu.SemaphoreType.DMA((10,)),
            pltpu.SemaphoreType.DMA((SWEEPS, 2, 2)),
            pltpu.SemaphoreType.DMA((SWEEPS, 2, 2)),
            pltpu.SemaphoreType.DMA((6,)),
            pltpu.SemaphoreType.DMA((6,)),
        ],
        compiler_params=pltpu.CompilerParams(collective_id=0, has_side_effects=True),
    )(
        warm, humid, cx, cy, gas[None], drop[None], sw[None], lw[None], flags, slots,
    )
    t, m, rates = pl.pallas_call(
        hand_on,
        out_shape=tuple(jax.ShapeDtypeStruct(a.shape, F32) for a in (t, m, rates)),
        in_specs=[vmem] * 3,
        out_specs=(vmem,) * 3,
    )(t, m, rates)
    return t, m, rates.T


def solution(mesh):
    assert mesh.shape["grp"] == 2
    in_specs = (
        P("grp", "gx", "gy"), P("grp", "gx", "gy"), P(), P(), P(), P(), P(), P(),
        P(("grp", "gx", "gy"), None), P("gx", "gy"),
    )
    out_specs = (P("grp", "gx", "gy"), P("grp", "gx", "gy"), P(("grp", "gx", "gy"), None))
    return jax.shard_map(
        functools.partial(body, mesh.shape["gx"], mesh.shape["gy"]),
        mesh=mesh, in_specs=in_specs, out_specs=out_specs, check_vma=False,
    )
```

profile of v0, /device:TPU:0, one launch (start us, length us, event | category | flops | bytes accessed | tf_op | source)
XLA Modules:
  0.0 54.9 jit_solution(10352619479121035726)
XLA Ops:
  0.6 52.4 %shard_map.121 = (f32[32,16,128]{2,1,0:T(8,128)}, f32[32,16,128]{2,1,0:T(8,128)}, f32[64,256]{1,0:T(8,128)}) custom-call(f32[32,16,128]{2,1,0:T(8,128)} %warm_in.1, f32[32,16,128]{2,1,0:T(8,128)} %humid_in.1, f32[64]{0:T(128)} %cx_ref.1, f32[64]{0:T(128)} %cy_ref.1, f32[1,112]{1,0:T(1,128)} %bitcast.7, f32[1,112]{1,0:T(1,128)} %bitcast.8, f32[1,112]{1,0:T(1,128)} %bitcast.9, ...), custom_call_target="tpu_custom_call" | custom-call | tf_op jit(solution)/shard_map/pallas_call | solution.py:349
  53.1 1.9 %shard_map.122 = (f32[32,16,128]{2,1,0:T(8,128)}, f32[32,16,128]{2,1,0:T(8,128)}, f32[64,256]{1,0:T(8,128)}) custom-call(f32[32,16,128]{2,1,0:T(8,128)} %get-tuple-element.9.t_in, f32[32,16,128]{2,1,0:T(8,128)} %get-tuple-element.10.m_in, f32[64,256]{1,0:T(8,128)} %get-tuple-element.11.r_in), custom_call_target="tpu_custom_call" | custom-call | tf_op jit(solution)/shard_map/pallas_call | solution.py:388
where the time goes:
time: 55.1 us; the launch traced here: 54.9 us
  Pallas kernels  54.3 us (99%)
  between operations  0.64 us (1%)
    pallas_call x1, Pallas kernels, body(): pl.pallas_call(functools.partial(kernel, n_gx, n_gy, L, R, C, S, B, G), o...  52.4 us
    pallas_call x1, Pallas kernels, body(): pl.pallas_call(hand_on, out_shape=tuple((jax.ShapeDtypeStruct(a.shape, F3...  1.85 us

commit v1 on v0

--- a/solution.py
+++ b/solution.py
@@ -381,7 +381,7 @@
             pltpu.SemaphoreType.DMA((6,)),
             pltpu.SemaphoreType.DMA((6,)),
         ],
-        compiler_params=pltpu.CompilerParams(collective_id=0, has_side_effects=True),
+        compiler_params=pltpu.CompilerParams(collective_id=0, has_side_effects=True, vmem_limit_bytes=32*1024*1024),
     )(
         warm, humid, cx, cy, gas[None], drop[None], sw[None], lw[None], flags, slots,
     )
@@ -389,7 +389,7 @@
         hand_on,
         out_shape=tuple(jax.ShapeDtypeStruct(a.shape, F32) for a in (t, m, rates)),
         in_specs=[vmem] * 3,
-        out_specs=(vmem,) * 3,
+        out_specs=(vmem,) * 3, compiler_params=pltpu.CompilerParams(vmem_limit_bytes=8*1024*1024),
     )(t, m, rates)
     return t, m, rates.T
 

time: 55.1 us -> 55.7 us (1.011)
  local copies, waits for them, and re-layouts: 0 us -> 3.43 us
  Pallas kernels: 54.3 us -> 51.3 us
    unnamed x0 -> x20, local copies, waits for them, and re-layouts: none -> 3.43 us
    pallas_call x1, Pallas kernels: 52.4 us -> 50.5 us  [body(): pl.pallas_call(functools.partial(kernel, n_gx, n_gy, L, R, C, S, B, G), o...]
    pallas_call x1, Pallas kernels: 1.85 us -> 0.84 us  [body(): pl.pallas_call(hand_on, out_shape=tuple((jax.ShapeDtypeStruct(a.shape, F3...]
where the time goes in v1:
time: 55.7 us; the launch traced here: 55.5 us
  Pallas kernels  51.3 us (92%)
  local copies, waits for them, and re-layouts  3.43 us (6%)
  between operations  0.7 us (1%)
    pallas_call x1, Pallas kernels, body(): pl.pallas_call(functools.partial(kernel, n_gx, n_gy, L, R, C, S, B, G), o...  50.5 us
    unnamed x20, local copies, waits for them, and re-layouts  3.43 us

profile of v1, /device:TPU:0, one launch (start us, length us, event | category | flops | bytes accessed | tf_op | source)
XLA Modules:
  0.0 55.5 jit_solution(7198162507204201886)
XLA Ops:
  0.6 0.0 copy-start.3
  0.6 0.0 copy-start.7
  0.7 0.0 copy-start.8
  0.7 0.0 copy-start.9
  0.7 0.0 copy-start.4
  0.7 0.0 copy-start.5
  0.7 0.0 copy-start.6
  0.7 0.6 %copy-done.3 = s32[8,64]{1,0:T(8,128)S(1)} copy-done((s32[8,64]{1,0:T(8,128)S(1)}, s32[8,64]{1,0:T(8,128)}, u32[]{:S(2)}) %copy-start.3) | copy-done | bytes 2072
  1.3 0.0 copy-done.7
  1.3 0.0 copy-done.8
  1.3 0.0 copy-done.9
  1.3 0.0 copy-done.4
  1.4 0.0 copy-done.5
  1.4 0.0 copy-done.6
  1.4 0.0 copy-start
  1.4 0.9 %copy-done = f32[32,16,128]{2,1,0:T(8,128)S(1)} copy-done((f32[32,16,128]{2,1,0:T(8,128)S(1)}, f32[32,16,128]{2,1,0:T(8,128)}, u32[]{:S(2)}) %copy-start) | copy-done | bytes 262168
  2.3 0.0 copy-start.1
  2.3 0.9 %copy-done.1 = f32[32,16,128]{2,1,0:T(8,128)S(1)} copy-done((f32[32,16,128]{2,1,0:T(8,128)S(1)}, f32[32,16,128]{2,1,0:T(8,128)}, u32[]{:S(2)}) %copy-start.1) | copy-done | bytes 262168
  3.3 0.0 copy-start.2
  3.3 0.8 %copy-done.2 = s32[256,64]{0,1:T(8,128)S(1)} copy-done((s32[256,64]{0,1:T(8,128)S(1)}, s32[256,64]{0,1:T(8,128)}, u32[]{:S(2)}) %copy-start.2) | copy-done | bytes 65560
  4.1 50.5 %shard_map.121 = (f32[32,16,128]{2,1,0:T(8,128)S(1)}, f32[32,16,128]{2,1,0:T(8,128)S(1)}, f32[64,256]{1,0:T(8,128)S(1)}) custom-call(f32[32,16,128]{2,1,0:T(8,128)S(1)} %copy-done, f32[32,16,128]{2,1,0:T(8,128)S(1)} %copy-done.1, f32[64]{0:T(128)S(1)} %copy-done.4, f32[64]{0:T(128)S(1)} %copy-done.5, f32[1,112]{1,0:T(1,128)S(1)} %bitcast.7, ...), custom_call_target="tpu_custom_call" | custom-call | tf_op jit(solution)/shard_map/pallas_call | solution.py:349
  54.6 0.8 %shard_map.122 = (f32[32,16,128]{2,1,0:T(8,128)}, f32[32,16,128]{2,1,0:T(8,128)}, f32[64,256]{1,0:T(8,128)}) custom-call(f32[32,16,128]{2,1,0:T(8,128)S(1)} %get-tuple-element.9.t_in, f32[32,16,128]{2,1,0:T(8,128)S(1)} %get-tuple-element.10.m_in, f32[64,256]{1,0:T(8,128)S(1)} %get-tuple-element.11.r_in), custom_call_target="tpu_custom_call" | custom-call | tf_op jit(solution)/shard_map/pallas_call | solution.py:388
Async XLA Ops:
  0.6 0.7 %copy-start.3 = (s32[8,64]{1,0:T(8,128)S(1)}, s32[8,64]{1,0:T(8,128)}, u32[]{:S(2)}) copy-start(s32[8,64]{1,0:T(8,128)} %slot_ref.1) | copy-start | bytes 6148
  0.6 0.7 %copy-start.7 = (f32[112]{0:T(128)S(1)}, f32[112]{0:T(128)}, u32[]{:S(2)}) copy-start(f32[112]{0:T(128)} %param.15) | copy-start | bytes 1348
  0.7 0.7 %copy-start.8 = (f32[112]{0:T(128)S(1)}, f32[112]{0:T(128)}, u32[]{:S(2)}) copy-start(f32[112]{0:T(128)} %param.16) | copy-start | bytes 1348
  0.7 0.7 %copy-start.9 = (f32[112]{0:T(128)S(1)}, f32[112]{0:T(128)}, u32[]{:S(2)}) copy-start(f32[112]{0:T(128)} %param.17) | copy-start | bytes 1348
  0.7 0.7 %copy-start.4 = (f32[64]{0:T(128)S(1)}, f32[64]{0:T(128)}, u32[]{:S(2)}) copy-start(f32[64]{0:T(128)} %cx_ref.1) | copy-start | bytes 772
  0.7 0.7 %copy-start.5 = (f32[64]{0:T(128)S(1)}, f32[64]{0:T(128)}, u32[]{:S(2)}) copy-start(f32[64]{0:T(128)} %cy_ref.1) | copy-start | bytes 772
  0.7 0.7 %copy-start.6 = (f32[112]{0:T(128)S(1)}, f32[112]{0:T(128)}, u32[]{:S(2)}) copy-start(f32[112]{0:T(128)} %param.14) | copy-start | bytes 1348
  1.4 0.9 %copy-start = (f32[32,16,128]{2,1,0:T(8,128)S(1)}, f32[32,16,128]{2,1,0:T(8,128)}, u32[]{:S(2)}) copy-start(f32[32,16,128]{2,1,0:T(8,128)} %warm_in.1) | copy-start | bytes 786436
  2.3 0.9 %copy-start.1 = (f32[32,16,128]{2,1,0:T(8,128)S(1)}, f32[32,16,128]{2,1,0:T(8,128)}, u32[]{:S(2)}) copy-start(f32[32,16,128]{2,1,0:T(8,128)} %humid_in.1) | copy-start | bytes 786436
  3.3 0.8 %copy-start.2 = (s32[256,64]{0,1:T(8,128)S(1)}, s32[256,64]{0,1:T(8,128)}, u32[]{:S(2)}) copy-start(s32[256,64]{0,1:T(8,128)} %param.18) | copy-start | bytes 196612

commit v2 on v0

--- a/solution.py
+++ b/solution.py
@@ -25,7 +25,7 @@
     return hi, lo
 
 
-def kernel(
+def wide_kernel(
     n_gx, n_gy, L, R, C, S, B, G,
     warm_in, humid_in, cx_ref, cy_ref, gas_ref, drop_ref, sw_ref, lw_ref, flags_ref, slot_ref,
     t_out, m_out, rates_out,
@@ -335,7 +335,7 @@
     r_out[...] = r_in[...]
 
 
-def body(n_gx, n_gy, warm, humid, cx, cy, gas, drop, sw, lw, flags, slots):
+def wide_body(n_gx, n_gy, warm, humid, cx, cy, gas, drop, sw, lw, flags, slots):
     L, R, C = warm.shape
     S = slots.shape[0] * slots.shape[1]
     B = flags.shape[0]
@@ -347,7 +347,7 @@
     vmem = pl.BlockSpec(memory_space=pltpu.VMEM)
     smem = pl.BlockSpec(memory_space=pltpu.SMEM)
     t, m, rates = pl.pallas_call(
-        functools.partial(kernel, n_gx, n_gy, L, R, C, S, B, G),
+        functools.partial(wide_kernel, n_gx, n_gy, L, R, C, S, B, G),
         out_shape=(
             jax.ShapeDtypeStruct((L, R, C), F32),
             jax.ShapeDtypeStruct((L, R, C), F32),
@@ -394,6 +394,417 @@
     return t, m, rates.T
 
 
+CHUNK = 2
+PAD = 8
+
+
+def pair_kernel(
+    n_gx, L, R, C, S, B, G,
+    warm_hbm, humid_hbm, cx_hbm, cy_hbm, gas_hbm, drop_hbm, sw_hbm, lw_hbm, flags_hbm, slot_hbm,
+    res, heat_out, rates_out,
+    fields, small, gpoint, flags_ref, slot_ref,
+    loc, buf0, buf1, fin, adv, lines, qt, packed, rad, coef, cloudy, absorber, theta, rates, heat, ucols,
+    hedge_send, hedge_recv, rows_send, rows_recv,
+    in_sem, pair_sem, lev_send_sem, lev_recv_sem, row_send_sem, row_recv_sem,
+    corner_send_sem, corner_recv_sem, misc_send_sem, misc_recv_sem,
+):
+    g = lax.axis_index("grp")
+    x = lax.axis_index("gx")
+    y = lax.axis_index("gy")
+    og = 1 - g
+    oy = 1 - y
+    xn, xp = lax.rem(x + 1, n_gx), lax.rem(x + n_gx - 1, n_gx)
+    LE = L + M
+    RE = R + 2 * M
+    RI = R // 2
+    NC = M // CHUNK
+    bufs = (buf0, buf1)
+
+    barrier = pltpu.get_barrier_semaphore()
+    partners = [(g, x, oy), (og, x, 0), (og, x, 1)]
+    for gg in (g, og):
+        for xx in (xn, xp):
+            for yy in range(2):
+                partners.append((gg, xx, yy))
+    for dev in partners:
+        pl.semaphore_signal(barrier, inc=1, device_id=dev, device_id_type=MESH)
+
+    loads = []
+    pairs = [(warm_hbm, fields.at[0]), (humid_hbm, fields.at[1]), (slot_hbm, slot_ref)]
+    pairs += [(cx_hbm, small.at[0]), (cy_hbm, small.at[1])]
+    pairs += [(r, gpoint.at[q]) for q, r in enumerate((gas_hbm, drop_hbm, sw_hbm, lw_hbm))]
+    pairs += [(flags_hbm, flags_ref)]
+    for n, (src, dst) in enumerate(pairs):
+        c = pltpu.make_async_copy(src, dst, in_sem.at[n])
+        c.start()
+        loads.append(c)
+
+    def remote(src, dst, ss, rs, dev):
+        c = pltpu.make_async_remote_copy(
+            src_ref=src, dst_ref=dst, send_sem=ss, recv_sem=rs, device_id=dev, device_id_type=MESH
+        )
+        c.start()
+        return c
+
+    def arrived(dst, rs):
+        pltpu.make_async_remote_copy(
+            src_ref=dst, dst_ref=dst, send_sem=rs, recv_sem=rs, device_id=(g, x, oy), device_id_type=MESH
+        ).wait_recv()
+
+    zero = jnp.zeros((8, C), F32)
+    edge = jnp.zeros((RE, 8, C), F32)
+    for b in bufs:
+        for h in range(2):
+            b[h, :, 0:PAD, :] = edge
+            b[h, :, PAD + LE : PAD + LE + 8, :] = edge
+
+    for n in range(2):
+        loads[n].wait()
+    for f in range(2):
+        flat = fields.at[f].reshape(L * R, C)
+        for r in range(R):
+            loc[f, r] = flat[pl.ds(r, L, stride=R), :]
+
+    pl.semaphore_wait(barrier, 11)
+
+    own_dst = pl.multiple_of(PAD + M * g, 8)
+    lev_src = pl.multiple_of((L - M) * og, 8)
+    lev_dst = pl.multiple_of(PAD + L * g, 8)
+    pending = []
+    pending.append(remote(
+        loc.at[oy], buf0.at[y, M : M + R, pl.ds(own_dst, L), :],
+        pair_sem.at[0], pair_sem.at[1], (g, x, oy),
+    ))
+
+    def row_copies(c):
+        out = []
+        d1, d0 = CHUNK * c, CHUNK * (c + 1)
+        near = 1 if d0 == M else 0
+        for f in range(2):
+            for side, xx in ((0, xn), (1, xp)):
+                s0 = R - d0 if side == 0 else d1
+                t0 = M - d0 if side == 0 else M + R + d1
+                out.append(remote(
+                    loc.at[f, s0 : s0 + CHUNK], buf0.at[y, t0 : t0 + CHUNK, pl.ds(own_dst, L), :],
+                    row_send_sem.at[c, side, f], row_recv_sem.at[c, side, y], (g, xx, f),
+                ))
+                n = CHUNK - near
+                s1 = s0 + near if side == 0 else s0
+                t1 = t0 + near if side == 0 else t0
+                out.append(remote(
+                    loc.at[f, s1 : s1 + n, pl.ds(lev_src, M), :],
+                    buf0.at[y, t1 : t1 + n, pl.ds(lev_dst, M), :],
+                    corner_send_sem.at[c, side, f], corner_recv_sem.at[c, side, y], (og, xx, f),
+                ))
+        return out
+
+    def rows_arrived(c):
+        d1, d0 = CHUNK * c, CHUNK * (c + 1)
+        near = 1 if d0 == M else 0
+        n = CHUNK - near
+        for h in range(2):
+            for side in range(2):
+                t0 = M - d0 if side == 0 else M + R + d1
+                t1 = t0 + near if side == 0 else t0
+                arrived(buf0.at[h, t0 : t0 + CHUNK, pl.ds(own_dst, L), :], row_recv_sem.at[c, side, h])
+                arrived(buf0.at[h, t1 : t1 + n, pl.ds(lev_dst_in, M), :], corner_recv_sem.at[c, side, h])
+
+    lev_dst_in = pl.multiple_of(PAD + L * og, 8)
+    for c in range(NC):
+        pending += row_copies(c)
+
+    loads[2].wait()
+    half = slot_ref.shape[1]
+    slots = slot_ref[...]
+    rep = (
+        lax.broadcasted_iota(jnp.int32, (half, C), 1) // 2
+        == lax.broadcasted_iota(jnp.int32, (half, C), 0)
+    ).astype(F32).astype(BF)
+    s_hi = (slots // 16).astype(F32).astype(BF)
+    s_lo = (slots % 16).astype(F32).astype(BF)
+    slot_rep = (
+        16.0 * jnp.dot(s_hi, rep, preferred_element_type=F32)
+        + jnp.dot(s_lo, rep, preferred_element_type=F32)
+    ).astype(jnp.int32)
+    s_iota = lax.broadcasted_iota(jnp.int32, (S, C), 0)
+    for i in range(RI):
+        qt[:, i * C : (i + 1) * C] = jnp.where(s_iota == slot_rep[i : i + 1, :], 1.0, 0.0).astype(BF)
+    parts = []
+    for i in range(RI):
+        col = [loc[f, 2 * i] + loc[f, 2 * i + 1] for f in range(2)]
+        hi, lo = split_bf16(0.25 * jnp.concatenate(col, axis=0))
+        parts.append(jnp.concatenate([hi, lo], axis=0))
+    lhs = jnp.concatenate(parts, axis=1)
+    both = lax.dot_general(
+        lhs, qt[...], (((1,), (1,)), ((), ())), preferred_element_type=F32
+    )
+    both = both[: 2 * L] + both[2 * L :]
+    for h in range(2):
+        packed[h] = both[:, h * B : (h + 1) * B]
+    c_packed = remote(packed.at[og], rad.at[g], misc_send_sem.at[0], misc_recv_sem.at[0], (og, x, y))
+    for f in range(2):
+        pending.append(remote(
+            loc.at[f, :, pl.ds(lev_src, M), :], buf0.at[y, M : M + R, pl.ds(lev_dst, M), :],
+            lev_send_sem.at[f], lev_recv_sem.at[y], (og, x, f),
+        ))
+    rad[g] = packed[g]
+    buf0[y, M : M + R, pl.ds(own_dst, L), :] = loc[y]
+
+    for n in range(3, len(loads)):
+        loads[n].wait()
+    for q in range(2):
+        lines[q] = jnp.broadcast_to(small[q], (C, 2 * L)).T
+    for q in range(2):
+        part = 0.5 * lines[q, pl.ds(pl.multiple_of((L - M) * g, 8), LE), :]
+        adv[2 * q] = NU_H - part
+        adv[2 * q + 1] = NU_H + part
+    log2e = 1.0 / math.log(2.0)
+    for q, scale in enumerate((-log2e, -log2e, 1.0, 1.0)):
+        coef[q] = jnp.broadcast_to(gpoint[q] * scale, (128, G)).T
+    for hb in range(B // 128):
+        cloudy[hb] = flags_ref[:, hb * 128 : (hb + 1) * 128].astype(F32)
+
+    c_packed.wait()
+    for o in range(2):
+        mo = rad[o, L : 2 * L, :]
+        soft = jnp.maximum(mo, 0.0) + jnp.log1p(jnp.exp(-jnp.abs(mo)))
+        for hb in range(B // 128):
+            absorber[hb, o * L : (o + 1) * L, :] = soft[:, hb * 128 : (hb + 1) * 128]
+            theta[hb, o * L : (o + 1) * L, :] = rad[o, 0:L, hb * 128 : (hb + 1) * 128]
+
+    GB = G // 8
+    norm = 4.0 / G
+    for hb in range(B // 128):
+        for o in range(2):
+            def level(l, flux, o=o, hb=hb):
+                lg = l + o * L
+                a = jnp.broadcast_to(absorber[hb, pl.ds(lg, 1), :], (8, 128))
+                c = jnp.broadcast_to(cloudy[hb, pl.ds(lg, 1), :], (8, 128))
+                th = 1.0 + 0.1 * theta[hb, pl.ds(lg, 1), :]
+                sw = lw = None
+                new = []
+                for q in range(GB):
+                    rows = slice(8 * q, 8 * q + 8)
+                    d = 1.0 - jnp.exp2(a * coef[0, rows, :] + c * coef[1, rows, :])
+                    s = flux[q] * d
+                    w = coef[3, rows, :] * d
+                    sw = s if sw is None else sw + s
+                    lw = w if lw is None else lw + w
+                    new.append(flux[q] - s)
+                total = jnp.sum(sw - lw * th, axis=0, keepdims=True) * norm
+                rates[o, hb, pl.ds(l, 1), :] = total
+                return tuple(new)
+
+            if o == 0:
+                flux = tuple(coef[2, 8 * q : 8 * q + 8, :] for q in range(GB))
+            flux = lax.fori_loop(0, L, level, flux, unroll=2)
+    c_heat = remote(rates.at[og], heat.at[g], misc_send_sem.at[1], misc_recv_sem.at[1], (og, x, y))
+    heat[g] = rates[g]
+    for o in range(2):
+        for hb in range(B // 128):
+            rates_out[o * L : (o + 1) * L, hb * 128 : (hb + 1) * 128] = rates[o, hb]
+
+    def stencil(k, i0, n):
+        src, dst = bufs[(k - 1) % 2], bufs[k % 2]
+        lane = lax.broadcasted_iota(jnp.int32, (n * LE, C), 1)
+        span = [src[h, i0 - 1 : i0 + n + 1, PAD : PAD + LE, :] for h in range(2)]
+        mid = [v[1 : n + 1].reshape(n * LE, C) for v in span]
+        right = [pltpu.roll(v, 1, 1) for v in mid]
+        left = [pltpu.roll(v, C - 1, 1) for v in mid]
+        for h in range(2):
+            prev = jnp.where(lane == 0, right[1 - h], right[h]).reshape(n, LE, C)
+            nxt = jnp.where(lane == C - 1, left[1 - h], left[h]).reshape(n, LE, C)
+            up = src[h, i0 : i0 + n, PAD - 1 : PAD + LE - 1, :]
+            down = src[h, i0 : i0 + n, PAD + 1 : PAD + LE + 1, :]
+            new = (
+                (1.0 - 4.0 * NU_H - 2.0 * NU_V) * span[h][1 : n + 1]
+                + NU_V * (up + down)
+                + adv[0][None] * span[h][2 : n + 2]
+                + adv[1][None] * span[h][0:n]
+                + adv[2][None] * nxt
+                + adv[3][None] * prev
+            )
+            if k == SWEEPS:
+                fin[h, i0 - M : i0 - M + n] = new
+            else:
+                dst[h, i0 : i0 + n, PAD : PAD + LE, :] = new
+
+    def strip(c):
+        h = CHUNK * (c + 1)
+        for k in range(1, SWEEPS + 1):
+            stencil(k, M + k - h, CHUNK)
+            stencil(k, M + R - (k - h) - CHUNK, CHUNK)
+
+    arrived(buf0.at[oy, M : M + R, pl.ds(own_dst, L), :], pair_sem.at[1])
+    for h in range(2):
+        arrived(buf0.at[h, M : M + R, pl.ds(lev_dst_in, M), :], lev_recv_sem.at[h])
+    for k in range(1, SWEEPS):
+        i0, i1 = M + k, M + R - k
+        while i0 < i1:
+            n = min(2, i1 - i0)
+            stencil(k, i0, n)
+            i0 += n
+
+    c_heat.wait()
+    hi, lo = split_bf16(jnp.concatenate([heat[h, hb] for h in range(2) for hb in range(B // 128)], axis=1))
+    spread = jnp.dot(jnp.concatenate([hi, lo], axis=0), qt[...], preferred_element_type=F32)
+    spread = spread[:L] + spread[L:]
+    lane = lax.broadcasted_iota(jnp.int32, (8, C), 1)
+    LT = L // 8
+    ehi = zero
+    elo = zero
+    for i in range(RI):
+        ui = spread[:, i * C : (i + 1) * C]
+        ucols[i] = ui
+        for t in range(LT):
+            k = i * LT + t
+            turned = pltpu.roll(ui[8 * t : 8 * t + 8, :], (k + 1) % C, 1)
+            ehi = jnp.where(lane == k, turned, ehi)
+            elo = jnp.where(lane == (k + 1) % C, turned, elo)
+    hedge_send[0] = ehi
+    hedge_send[1] = elo
+    c_he = [
+        remote(hedge_send.at[n], hedge_recv.at[n], misc_send_sem.at[2 + n], misc_recv_sem.at[2 + n], (g, x, oy))
+        for n in range(2)
+    ]
+
+    rows_arrived(0)
+    strip(0)
+
+    for c in c_he:
+        c.wait()
+    from_left = hedge_recv[0]
+    from_right = hedge_recv[1]
+    even = lane % 2 == 0
+    for i in range(RI):
+        for t in range(LT):
+            k = i * LT + t
+            v = ucols[i, 8 * t : 8 * t + 8, :]
+            prev = jnp.where(lane == 0, pltpu.roll(from_left, (C - k) % C, 1), pltpu.roll(v, 1, 1))
+            nxt = jnp.where(lane == C - 1, pltpu.roll(from_right, (2 * C - 2 - k) % C, 1), pltpu.roll(v, C - 1, 1))
+            w = 0.75 * v + 0.25 * jnp.where(even, prev, nxt)
+            ucols[i, 8 * t : 8 * t + 8, :] = w
+            if i == 0:
+                rows_send[0, 8 * t : 8 * t + 8, :] = w
+            if i == RI - 1:
+                rows_send[1, 8 * t : 8 * t + 8, :] = w
+    c_rows = [
+        remote(rows_send.at[0], rows_recv.at[0], misc_send_sem.at[4], misc_recv_sem.at[4], (g, xp, y)),
+        remote(rows_send.at[1], rows_recv.at[1], misc_send_sem.at[5], misc_recv_sem.at[5], (g, xn, y)),
+    ]
+
+    for c in range(1, NC):
+        rows_arrived(c)
+        strip(c)
+
+    mine = pl.multiple_of(M * g, 8)
+    c_fin = remote(
+        fin.at[oy, :, pl.ds(mine, L), :], res.at[y], pair_sem.at[2], pair_sem.at[3], (g, x, oy)
+    )
+    res[y] = fin[y, :, pl.ds(mine, L), :]
+    for c in c_rows:
+        c.wait()
+    for i in range(RI):
+        v = ucols[i]
+        above = rows_recv[1] if i == 0 else ucols[i - 1]
+        below = rows_recv[0] if i == RI - 1 else ucols[i + 1]
+        heat_out[2 * i] = HEATING_INTERVAL * (0.75 * v + 0.25 * above)
+        heat_out[2 * i + 1] = HEATING_INTERVAL * (0.75 * v + 0.25 * below)
+    for c in pending:
+        c.wait_send()
+    c_fin.wait_send()
+    arrived(res.at[oy], pair_sem.at[3])
+
+
+def settle(res, heat, r_in, t_out, m_out, r_out):
+    L, R, C = t_out.shape
+    t_flat = t_out.reshape(L * R, C)
+    m_flat = m_out.reshape(L * R, C)
+    for r in range(R):
+        t_flat[pl.ds(r, L, stride=R), :] = res[0, r] + heat[r]
+        m_flat[pl.ds(r, L, stride=R), :] = res[1, r]
+    r_out[...] = r_in[...]
+
+
+def pair_body(n_gx, n_gy, warm, humid, cx, cy, gas, drop, sw, lw, flags, slots):
+    L, R, C = warm.shape
+    S = slots.shape[0] * slots.shape[1]
+    B = flags.shape[0]
+    flags = flags.T
+    G = gas.shape[0]
+    LE = L + M
+    LP = PAD + LE + 8
+    RE = R + 2 * M
+    NC = M // CHUNK
+    vmem = pl.BlockSpec(memory_space=pltpu.VMEM)
+    hbm = pl.BlockSpec(memory_space=pltpu.HBM)
+    res, heat, rates = pl.pallas_call(
+        functools.partial(pair_kernel, n_gx, L, R, C, S, B, G),
+        out_shape=(
+            jax.ShapeDtypeStruct((2, R, L, C), F32),
+            jax.ShapeDtypeStruct((R, L, C), F32),
+            jax.ShapeDtypeStruct((2 * L, B), F32),
+        ),
+        in_specs=[hbm] * 10,
+        out_specs=(vmem, vmem, vmem),
+        scratch_shapes=[
+            pltpu.VMEM((2, L, R, C), F32),
+            pltpu.VMEM((2, 1, 2 * L), F32),
+            pltpu.VMEM((4, 1, G), F32),
+            pltpu.VMEM((2 * L, B), jnp.int32),
+            pltpu.VMEM(slots.shape, jnp.int32),
+            pltpu.VMEM((2, R, L, C), F32),
+            pltpu.VMEM((2, RE, LP, C), F32),
+            pltpu.VMEM((2, RE, LP, C), F32),
+            pltpu.VMEM((2, R, LE, C), F32),
+            pltpu.VMEM((4, LE, C), F32),
+            pltpu.VMEM((2, 2 * L, C), F32),
+            pltpu.VMEM((S, (R // 2) * C), BF),
+            pltpu.VMEM((2, 2 * L, B), F32),
+            pltpu.VMEM((2, 2 * L, B), F32),
+            pltpu.VMEM((4, G, 128), F32),
+            pltpu.VMEM((B // 128, 2 * L, 128), F32),
+            pltpu.VMEM((B // 128, 2 * L, 128), F32),
+            pltpu.VMEM((B // 128, 2 * L, 128), F32),
+            pltpu.VMEM((2, B // 128, L, 128), F32),
+            pltpu.VMEM((2, B // 128, L, 128), F32),
+            pltpu.VMEM((R // 2, L, C), F32),
+            pltpu.VMEM((2, 8, C), F32),
+            pltpu.VMEM((2, 8, C), F32),
+            pltpu.VMEM((2, L, C), F32),
+            pltpu.VMEM((2, L, C), F32),
+            pltpu.SemaphoreType.DMA((10,)),
+            pltpu.SemaphoreType.DMA((4,)),
+            pltpu.SemaphoreType.DMA((2,)),
+            pltpu.SemaphoreType.DMA((2,)),
+            pltpu.SemaphoreType.DMA((NC, 2, 2)),
+            pltpu.SemaphoreType.DMA((NC, 2, 2)),
+            pltpu.SemaphoreType.DMA((NC, 2, 2)),
+            pltpu.SemaphoreType.DMA((NC, 2, 2)),
+            pltpu.SemaphoreType.DMA((6,)),
+            pltpu.SemaphoreType.DMA((6,)),
+        ],
+        compiler_params=pltpu.CompilerParams(
+            collective_id=0, has_side_effects=True, vmem_limit_bytes=32 * 1024 * 1024
+        ),
+    )(*(
+        pltpu.with_memory_space_constraint(a, pltpu.HBM)
+        for a in (warm, humid, cx[None], cy[None], gas[None], drop[None], sw[None], lw[None], flags, slots)
+    ))
+    t, m, rates = pl.pallas_call(
+        settle,
+        out_shape=(
+            jax.ShapeDtypeStruct((L, R, C), F32),
+            jax.ShapeDtypeStruct((L, R, C), F32),
+            jax.ShapeDtypeStruct((2 * L, B), F32),
+        ),
+        in_specs=[vmem] * 3,
+        out_specs=(vmem,) * 3,
+        compiler_params=pltpu.CompilerParams(vmem_limit_bytes=8 * 1024 * 1024),
+    )(res, heat, rates)
+    return t, m, rates.T
+
+
 def solution(mesh):
     assert mesh.shape["grp"] == 2
     in_specs = (
@@ -401,7 +812,8 @@
         P(("grp", "gx", "gy"), None), P("gx", "gy"),
     )
     out_specs = (P("grp", "gx", "gy"), P("grp", "gx", "gy"), P(("grp", "gx", "gy"), None))
+    paired = mesh.shape["gy"] == 2 and mesh.shape["gx"] > 2
     return jax.shard_map(
-        functools.partial(body, mesh.shape["gx"], mesh.shape["gy"]),
+        functools.partial(pair_body if paired else wide_body, mesh.shape["gx"], mesh.shape["gy"]),
         mesh=mesh, in_specs=in_specs, out_specs=out_specs, check_vma=False,
     )

time: 55.1 us -> 28 us (0.51)
  Pallas kernels: 54.3 us -> 27.2 us
    pallas_call x2, Pallas kernels: 54.3 us -> 27.2 us  [the longest x1 26.2 us: pair_body(): pl.pallas_call(functools.partial(pair_kernel, n_gx, L, R, C, S, B, G), ou...]
where the time goes in v2:
time: 28 us; the launch traced here: 27.9 us
  Pallas kernels  27.2 us (97%)
  between operations  0.64 us (2%)
    pallas_call x1, Pallas kernels, pair_body(): pl.pallas_call(functools.partial(pair_kernel, n_gx, L, R, C, S, B, G), ou...  26.2 us
    pallas_call x1, Pallas kernels, pair_body(): pl.pallas_call(settle, out_shape=(jax.ShapeDtypeStruct((L, R, C), F32), j...  1.04 us

profile of v2, /device:TPU:0, one launch (start us, length us, event | category | flops | bytes accessed | tf_op | source)
XLA Modules:
  0.0 27.9 jit_solution(15600457223841501652)
XLA Ops:
  0.6 26.2 %shard_map.121 = (f32[2,16,32,128]{3,2,1,0:T(8,128)S(1)}, f32[16,32,128]{2,1,0:T(8,128)S(1)}, f32[64,256]{1,0:T(8,128)S(1)}) custom-call(f32[32,16,128]{2,1,0:T(8,128)} %warm_hbm.1, f32[32,16,128]{2,1,0:T(8,128)} %humid_hbm.1, f32[1,64]{1,0:T(1,128)} %bitcast.9, f32[1,64]{1,0:T(1,128)} %bitcast.10, f32[1,112]{1,0:T(1,128)} %bitcast.11, f32[1,112]{1,0:T(1,128)} %bitcast.12, ...), custom_call_target="tpu_custom_call" | custom-call | tf_op jit(solution)/shard_map/pallas_call | solution.py:741
  26.9 1.0 %shard_map.122 = (f32[32,16,128]{2,1,0:T(8,128)}, f32[32,16,128]{2,1,0:T(8,128)}, f32[64,256]{1,0:T(8,128)}) custom-call(f32[2,16,32,128]{3,2,1,0:T(8,128)S(1)} %get-tuple-element.9.res, f32[16,32,128]{2,1,0:T(8,128)S(1)} %get-tuple-element.10.heat, f32[64,256]{1,0:T(8,128)S(1)} %get-tuple-element.11.r_in), custom_call_target="tpu_custom_call" | custom-call | tf_op jit(solution)/shard_map/pallas_call | solution.py:794

commit v3 on v2

--- a/solution.py
+++ b/solution.py
@@ -394,7 +394,7 @@
     return t, m, rates.T
 
 
-CHUNK = 2
+CHUNK = 4
 PAD = 8
 
 
@@ -403,10 +403,8 @@
     warm_hbm, humid_hbm, cx_hbm, cy_hbm, gas_hbm, drop_hbm, sw_hbm, lw_hbm, flags_hbm, slot_hbm,
     res, heat_out, rates_out,
     fields, small, gpoint, flags_ref, slot_ref,
-    loc, buf0, buf1, fin, adv, lines, qt, packed, rad, coef, cloudy, absorber, theta, rates, heat, ucols,
-    hedge_send, hedge_recv, rows_send, rows_recv,
-    in_sem, pair_sem, lev_send_sem, lev_recv_sem, row_send_sem, row_recv_sem,
-    corner_send_sem, corner_recv_sem, misc_send_sem, misc_recv_sem,
+    loc, buf0, buf1, fin, adv, lines, qt, packed, rad, coef, cloudy, absorber, theta, passed, rates, heat, ucols, corner_send, corner_recv,
+    in_sem, pair_sem, lev_sem, row_send_sem, row_recv_sem, corner_sem, misc_sem,
 ):
     g = lax.axis_index("grp")
     x = lax.axis_index("gx")
@@ -420,6 +418,7 @@
     NC = M // CHUNK
     bufs = (buf0, buf1)
 
+    sub = lax.broadcasted_iota(jnp.int32, (M, C), 0)
     barrier = pltpu.get_barrier_semaphore()
     partners = [(g, x, oy), (og, x, 0), (og, x, 1)]
     for gg in (g, og):
@@ -430,7 +429,7 @@
         pl.semaphore_signal(barrier, inc=1, device_id=dev, device_id_type=MESH)
 
     loads = []
-    pairs = [(warm_hbm, fields.at[0]), (humid_hbm, fields.at[1]), (slot_hbm, slot_ref)]
+    pairs = [(slot_hbm, slot_ref), (warm_hbm, fields.at[0]), (humid_hbm, fields.at[1])]
     pairs += [(cx_hbm, small.at[0]), (cy_hbm, small.at[1])]
     pairs += [(r, gpoint.at[q]) for q, r in enumerate((gas_hbm, drop_hbm, sw_hbm, lw_hbm))]
     pairs += [(flags_hbm, flags_ref)]
@@ -446,74 +445,24 @@
         c.start()
         return c
 
-    def arrived(dst, rs):
-        pltpu.make_async_remote_copy(
-            src_ref=dst, dst_ref=dst, send_sem=rs, recv_sem=rs, device_id=(g, x, oy), device_id_type=MESH
-        ).wait_recv()
-
-    zero = jnp.zeros((8, C), F32)
+    def matching(ref, sem):
+        return pltpu.make_async_remote_copy(
+            src_ref=ref, dst_ref=ref, send_sem=sem, recv_sem=sem, device_id=(g, x, oy), device_id_type=MESH
+        )
+
+    def arrived(ref, sem):
+        matching(ref, sem).wait_recv()
+
+    def left(ref, sem):
+        matching(ref, sem).wait_send()
+
     edge = jnp.zeros((RE, 8, C), F32)
     for b in bufs:
         for h in range(2):
             b[h, :, 0:PAD, :] = edge
             b[h, :, PAD + LE : PAD + LE + 8, :] = edge
 
-    for n in range(2):
-        loads[n].wait()
-    for f in range(2):
-        flat = fields.at[f].reshape(L * R, C)
-        for r in range(R):
-            loc[f, r] = flat[pl.ds(r, L, stride=R), :]
-
-    pl.semaphore_wait(barrier, 11)
-
-    own_dst = pl.multiple_of(PAD + M * g, 8)
-    lev_src = pl.multiple_of((L - M) * og, 8)
-    lev_dst = pl.multiple_of(PAD + L * g, 8)
-    pending = []
-    pending.append(remote(
-        loc.at[oy], buf0.at[y, M : M + R, pl.ds(own_dst, L), :],
-        pair_sem.at[0], pair_sem.at[1], (g, x, oy),
-    ))
-
-    def row_copies(c):
-        out = []
-        d1, d0 = CHUNK * c, CHUNK * (c + 1)
-        near = 1 if d0 == M else 0
-        for f in range(2):
-            for side, xx in ((0, xn), (1, xp)):
-                s0 = R - d0 if side == 0 else d1
-                t0 = M - d0 if side == 0 else M + R + d1
-                out.append(remote(
-                    loc.at[f, s0 : s0 + CHUNK], buf0.at[y, t0 : t0 + CHUNK, pl.ds(own_dst, L), :],
-                    row_send_sem.at[c, side, f], row_recv_sem.at[c, side, y], (g, xx, f),
-                ))
-                n = CHUNK - near
-                s1 = s0 + near if side == 0 else s0
-                t1 = t0 + near if side == 0 else t0
-                out.append(remote(
-                    loc.at[f, s1 : s1 + n, pl.ds(lev_src, M), :],
-                    buf0.at[y, t1 : t1 + n, pl.ds(lev_dst, M), :],
-                    corner_send_sem.at[c, side, f], corner_recv_sem.at[c, side, y], (og, xx, f),
-                ))
-        return out
-
-    def rows_arrived(c):
-        d1, d0 = CHUNK * c, CHUNK * (c + 1)
-        near = 1 if d0 == M else 0
-        n = CHUNK - near
-        for h in range(2):
-            for side in range(2):
-                t0 = M - d0 if side == 0 else M + R + d1
-                t1 = t0 + near if side == 0 else t0
-                arrived(buf0.at[h, t0 : t0 + CHUNK, pl.ds(own_dst, L), :], row_recv_sem.at[c, side, h])
-                arrived(buf0.at[h, t1 : t1 + n, pl.ds(lev_dst_in, M), :], corner_recv_sem.at[c, side, h])
-
-    lev_dst_in = pl.multiple_of(PAD + L * og, 8)
-    for c in range(NC):
-        pending += row_copies(c)
-
-    loads[2].wait()
+    loads[0].wait()
     half = slot_ref.shape[1]
     slots = slot_ref[...]
     rep = (
@@ -529,6 +478,39 @@
     s_iota = lax.broadcasted_iota(jnp.int32, (S, C), 0)
     for i in range(RI):
         qt[:, i * C : (i + 1) * C] = jnp.where(s_iota == slot_rep[i : i + 1, :], 1.0, 0.0).astype(BF)
+    for n in range(1, 3):
+        loads[n].wait()
+    for f in range(2):
+        flat = fields.at[f].reshape(L * R, C)
+        for r in range(R):
+            loc[f, r] = flat[pl.ds(r, L, stride=R), :]
+
+    pl.semaphore_wait(barrier, 11)
+
+    own_dst = pl.multiple_of(PAD + M * g, 8)
+    lev_src = pl.multiple_of((L - M) * og, 8)
+    lev_own = pl.multiple_of(PAD + M * g + (L - M) * og, 8)
+    lev_dst = pl.multiple_of(PAD + L * g, 8)
+    lev_in = pl.multiple_of(PAD + L * og, 8)
+
+    lead = jnp.where(x == n_gx - 1, 0, 1)
+    for turn in range(2):
+        side = lead if turn == 0 else 1 - lead
+        up = side == 0
+        xx = jnp.where(up, xn, xp)
+        for c in range(NC):
+            d1, d0 = CHUNK * c, CHUNK * (c + 1)
+            s0 = jnp.where(up, R - d0, d1)
+            t0 = jnp.where(up, M - d0, M + R + d1)
+            for f in range(2):
+                remote(
+                    loc.at[f, pl.ds(s0, CHUNK)], buf0.at[y, pl.ds(t0, CHUNK), pl.ds(own_dst, L), :],
+                    row_send_sem.at[0], row_recv_sem.at[c], (g, xx, f),
+                )
+
+    remote(
+        loc.at[oy], buf0.at[y, M : M + R, pl.ds(own_dst, L), :], pair_sem.at[0], pair_sem.at[1], (g, x, oy)
+    )
     parts = []
     for i in range(RI):
         col = [loc[f, 2 * i] + loc[f, 2 * i + 1] for f in range(2)]
@@ -541,12 +523,45 @@
     both = both[: 2 * L] + both[2 * L :]
     for h in range(2):
         packed[h] = both[:, h * B : (h + 1) * B]
-    c_packed = remote(packed.at[og], rad.at[g], misc_send_sem.at[0], misc_recv_sem.at[0], (og, x, y))
+    c_packed = remote(packed.at[og], rad.at[g], misc_sem.at[0], misc_sem.at[1], (og, x, y))
     for f in range(2):
-        pending.append(remote(
+        for side in range(2):
+            for j in range(M // 2):
+                d = j + 1
+                near, far = (R - d, R - M + d) if side == 0 else (d - 1, M - d - 1)
+                a = loc[f, near, pl.ds(lev_src, M), :]
+                b = loc[f, far, pl.ds(lev_src, M), :]
+                above = jnp.where(sub >= d, a, pltpu.roll(b, d, 0))
+                below = jnp.where(sub < M - d, a, pltpu.roll(b, M - d, 0))
+                corner_send[f, side, j] = jnp.where(g == 0, above, below)
+    for f in range(2):
+        for side, xx in ((0, xn), (1, xp)):
+            remote(
+                corner_send.at[f, side], corner_recv.at[y, side],
+                corner_sem.at[0], corner_sem.at[1], (og, xx, f),
+            )
+    for f in range(2):
+        remote(
             loc.at[f, :, pl.ds(lev_src, M), :], buf0.at[y, M : M + R, pl.ds(lev_dst, M), :],
-            lev_send_sem.at[f], lev_recv_sem.at[y], (og, x, f),
-        ))
+            lev_sem.at[0], lev_sem.at[1], (og, x, f),
+        )
+
+    def rows_arrived(c):
+        arrived(buf0.at[:, 0 : 2 * CHUNK, pl.ds(own_dst, L), :], row_recv_sem.at[c])
+
+    def corners_arrived():
+        arrived(corner_recv, corner_sem.at[1])
+        for h in range(2):
+            for side in range(2):
+                for j in range(M // 2):
+                    d = j + 1
+                    near, far = (M - d, d) if side == 0 else (M + R + d - 1, R + 2 * M - d - 1)
+                    v = corner_recv[h, side, j]
+                    buf0[h, near, pl.ds(lev_in, M), :] = v
+                    if near != far:
+                        back = jnp.where(g == 1, pltpu.roll(v, M - d, 0), pltpu.roll(v, d, 0))
+                        buf0[h, far, pl.ds(lev_in, M), :] = back
+
     rad[g] = packed[g]
     buf0[y, M : M + R, pl.ds(own_dst, L), :] = loc[y]
 
@@ -564,18 +579,24 @@
     for hb in range(B // 128):
         cloudy[hb] = flags_ref[:, hb * 128 : (hb + 1) * 128].astype(F32)
 
-    c_packed.wait()
+    GB = G // 8
+    HB = B // 128
+    norm = 4.0 / G
+    c_heat = pltpu.make_async_remote_copy(
+        src_ref=rates.at[og], dst_ref=heat.at[g], send_sem=misc_sem.at[2], recv_sem=misc_sem.at[3],
+        device_id=(og, x, y), device_id_type=MESH,
+    )
     for o in range(2):
+        @pl.when(og == o)
+        def _():
+            c_packed.wait()
+
         mo = rad[o, L : 2 * L, :]
         soft = jnp.maximum(mo, 0.0) + jnp.log1p(jnp.exp(-jnp.abs(mo)))
-        for hb in range(B // 128):
+        for hb in range(HB):
             absorber[hb, o * L : (o + 1) * L, :] = soft[:, hb * 128 : (hb + 1) * 128]
             theta[hb, o * L : (o + 1) * L, :] = rad[o, 0:L, hb * 128 : (hb + 1) * 128]
-
-    GB = G // 8
-    norm = 4.0 / G
-    for hb in range(B // 128):
-        for o in range(2):
+        for hb in range(HB):
             def level(l, flux, o=o, hb=hb):
                 lg = l + o * L
                 a = jnp.broadcast_to(absorber[hb, pl.ds(lg, 1), :], (8, 128))
@@ -595,14 +616,18 @@
                 rates[o, hb, pl.ds(l, 1), :] = total
                 return tuple(new)
 
+            start = coef.at[2] if o == 0 else passed.at[hb]
+            flux = tuple(start[8 * q : 8 * q + 8, :] for q in range(GB))
+            flux = lax.fori_loop(0, L, level, flux, unroll=2)
             if o == 0:
-                flux = tuple(coef[2, 8 * q : 8 * q + 8, :] for q in range(GB))
-            flux = lax.fori_loop(0, L, level, flux, unroll=2)
-    c_heat = remote(rates.at[og], heat.at[g], misc_send_sem.at[1], misc_recv_sem.at[1], (og, x, y))
+                for q in range(GB):
+                    passed[hb, 8 * q : 8 * q + 8, :] = flux[q]
+            rates_out[o * L : (o + 1) * L, hb * 128 : (hb + 1) * 128] = rates[o, hb]
+
+        @pl.when(og == o)
+        def _():
+            c_heat.start()
     heat[g] = rates[g]
-    for o in range(2):
-        for hb in range(B // 128):
-            rates_out[o * L : (o + 1) * L, hb * 128 : (hb + 1) * 128] = rates[o, hb]
 
     def stencil(k, i0, n):
         src, dst = bufs[(k - 1) % 2], bufs[k % 2]
@@ -636,8 +661,7 @@
             stencil(k, M + R - (k - h) - CHUNK, CHUNK)
 
     arrived(buf0.at[oy, M : M + R, pl.ds(own_dst, L), :], pair_sem.at[1])
-    for h in range(2):
-        arrived(buf0.at[h, M : M + R, pl.ds(lev_dst_in, M), :], lev_recv_sem.at[h])
+    arrived(buf0.at[:, M : M + R, pl.ds(lev_in, M), :], lev_sem.at[1])
     for k in range(1, SWEEPS):
         i0, i1 = M + k, M + R - k
         while i0 < i1:
@@ -649,70 +673,47 @@
     hi, lo = split_bf16(jnp.concatenate([heat[h, hb] for h in range(2) for hb in range(B // 128)], axis=1))
     spread = jnp.dot(jnp.concatenate([hi, lo], axis=0), qt[...], preferred_element_type=F32)
     spread = spread[:L] + spread[L:]
-    lane = lax.broadcasted_iota(jnp.int32, (8, C), 1)
-    LT = L // 8
-    ehi = zero
-    elo = zero
     for i in range(RI):
-        ui = spread[:, i * C : (i + 1) * C]
-        ucols[i] = ui
-        for t in range(LT):
-            k = i * LT + t
-            turned = pltpu.roll(ui[8 * t : 8 * t + 8, :], (k + 1) % C, 1)
-            ehi = jnp.where(lane == k, turned, ehi)
-            elo = jnp.where(lane == (k + 1) % C, turned, elo)
-    hedge_send[0] = ehi
-    hedge_send[1] = elo
-    c_he = [
-        remote(hedge_send.at[n], hedge_recv.at[n], misc_send_sem.at[2 + n], misc_recv_sem.at[2 + n], (g, x, oy))
-        for n in range(2)
-    ]
-
-    rows_arrived(0)
-    strip(0)
-
-    for c in c_he:
-        c.wait()
-    from_left = hedge_recv[0]
-    from_right = hedge_recv[1]
-    even = lane % 2 == 0
-    for i in range(RI):
-        for t in range(LT):
-            k = i * LT + t
-            v = ucols[i, 8 * t : 8 * t + 8, :]
-            prev = jnp.where(lane == 0, pltpu.roll(from_left, (C - k) % C, 1), pltpu.roll(v, 1, 1))
-            nxt = jnp.where(lane == C - 1, pltpu.roll(from_right, (2 * C - 2 - k) % C, 1), pltpu.roll(v, C - 1, 1))
-            w = 0.75 * v + 0.25 * jnp.where(even, prev, nxt)
-            ucols[i, 8 * t : 8 * t + 8, :] = w
-            if i == 0:
-                rows_send[0, 8 * t : 8 * t + 8, :] = w
-            if i == RI - 1:
-                rows_send[1, 8 * t : 8 * t + 8, :] = w
-    c_rows = [
-        remote(rows_send.at[0], rows_recv.at[0], misc_send_sem.at[4], misc_recv_sem.at[4], (g, xp, y)),
-        remote(rows_send.at[1], rows_recv.at[1], misc_send_sem.at[5], misc_recv_sem.at[5], (g, xn, y)),
-    ]
-
-    for c in range(1, NC):
+        ucols[y, 1 + i] = spread[:, i * C : (i + 1) * C]
+    for i, t, xx in ((1, RI + 1, xp), (RI, 0, xn)):
+        for yy in range(2):
+            remote(ucols.at[y, i], ucols.at[y, t], misc_sem.at[4], misc_sem.at[5], (g, xx, yy))
+    c_cols = remote(
+        ucols.at[y, 1 : RI + 1], ucols.at[y, 1 : RI + 1], misc_sem.at[6], misc_sem.at[7], (g, x, oy)
+    )
+
+    mine = pl.multiple_of(M * g, 8)
+    corners_arrived()
+    for c in range(NC):
         rows_arrived(c)
         strip(c)
-
-    mine = pl.multiple_of(M * g, 8)
-    c_fin = remote(
-        fin.at[oy, :, pl.ds(mine, L), :], res.at[y], pair_sem.at[2], pair_sem.at[3], (g, x, oy)
-    )
+        h = CHUNK * (c + 1)
+        for r in (M - h, R - M + h - CHUNK):
+            remote(
+                fin.at[oy, r : r + CHUNK, pl.ds(mine, L), :], res.at[y, r : r + CHUNK],
+                pair_sem.at[2], pair_sem.at[3], (g, x, oy),
+            )
     res[y] = fin[y, :, pl.ds(mine, L), :]
-    for c in c_rows:
-        c.wait()
+
+    c_cols.wait()
+    arrived(ucols.at[:, 0:2], misc_sem.at[5])
+    lane = lax.broadcasted_iota(jnp.int32, (L, C), 1)
+    even = lane % 2 == 0
+    cols = []
+    for i in range(RI + 2):
+        v, o = ucols[y, i], ucols[oy, i]
+        prev = jnp.where(lane == 0, pltpu.roll(o, 1, 1), pltpu.roll(v, 1, 1))
+        nxt = jnp.where(lane == C - 1, pltpu.roll(o, C - 1, 1), pltpu.roll(v, C - 1, 1))
+        cols.append(HEATING_INTERVAL * (0.75 * v + 0.25 * jnp.where(even, prev, nxt)))
     for i in range(RI):
-        v = ucols[i]
-        above = rows_recv[1] if i == 0 else ucols[i - 1]
-        below = rows_recv[0] if i == RI - 1 else ucols[i + 1]
-        heat_out[2 * i] = HEATING_INTERVAL * (0.75 * v + 0.25 * above)
-        heat_out[2 * i + 1] = HEATING_INTERVAL * (0.75 * v + 0.25 * below)
-    for c in pending:
-        c.wait_send()
-    c_fin.wait_send()
+        heat_out[2 * i] = 0.75 * cols[i + 1] + 0.25 * cols[i]
+        heat_out[2 * i + 1] = 0.75 * cols[i + 1] + 0.25 * cols[i + 2]
+    left(buf0.at[:, 0 : 2 * M, 0:L, :], row_send_sem.at[0])
+    left(corner_send, corner_sem.at[0])
+    left(buf0.at[:, 0:R, 0:M, :], lev_sem.at[0])
+    left(loc.at[oy], pair_sem.at[0])
+    left(ucols.at[:, 0:2], misc_sem.at[4])
+    left(res.at[oy], pair_sem.at[2])
     arrived(res.at[oy], pair_sem.at[3])
 
 
@@ -766,23 +767,19 @@
             pltpu.VMEM((B // 128, 2 * L, 128), F32),
             pltpu.VMEM((B // 128, 2 * L, 128), F32),
             pltpu.VMEM((B // 128, 2 * L, 128), F32),
+            pltpu.VMEM((B // 128, G, 128), F32),
             pltpu.VMEM((2, B // 128, L, 128), F32),
             pltpu.VMEM((2, B // 128, L, 128), F32),
-            pltpu.VMEM((R // 2, L, C), F32),
-            pltpu.VMEM((2, 8, C), F32),
-            pltpu.VMEM((2, 8, C), F32),
-            pltpu.VMEM((2, L, C), F32),
-            pltpu.VMEM((2, L, C), F32),
+            pltpu.VMEM((2, R // 2 + 2, L, C), F32),
+            pltpu.VMEM((2, 2, M // 2, M, C), F32),
+            pltpu.VMEM((2, 2, M // 2, M, C), F32),
             pltpu.SemaphoreType.DMA((10,)),
             pltpu.SemaphoreType.DMA((4,)),
             pltpu.SemaphoreType.DMA((2,)),
+            pltpu.SemaphoreType.DMA((1,)),
+            pltpu.SemaphoreType.DMA((NC,)),
             pltpu.SemaphoreType.DMA((2,)),
-            pltpu.SemaphoreType.DMA((NC, 2, 2)),
-            pltpu.SemaphoreType.DMA((NC, 2, 2)),
-            pltpu.SemaphoreType.DMA((NC, 2, 2)),
-            pltpu.SemaphoreType.DMA((NC, 2, 2)),
-            pltpu.SemaphoreType.DMA((6,)),
-            pltpu.SemaphoreType.DMA((6,)),
+            pltpu.SemaphoreType.DMA((8,)),
         ],
         compiler_params=pltpu.CompilerParams(
             collective_id=0, has_side_effects=True, vmem_limit_bytes=32 * 1024 * 1024

time: 28 us -> 24.6 us (0.88)
  Pallas kernels: 27.2 us -> 23.8 us
    pallas_call x1, Pallas kernels: 26.2 us -> 22.8 us  [pair_body(): pl.pallas_call(functools.partial(pair_kernel, n_gx, L, R, C, S, B, G), ou...]
where the time goes in v3:
time: 24.6 us; the launch traced here: 24.5 us
  Pallas kernels  23.8 us (97%)
  between operations  0.64 us (3%)
    pallas_call x1, Pallas kernels, pair_body(): pl.pallas_call(functools.partial(pair_kernel, n_gx, L, R, C, S, B, G), ou...  22.8 us
    pallas_call x1, Pallas kernels, pair_body(): pl.pallas_call(settle, out_shape=(jax.ShapeDtypeStruct((L, R, C), F32), j...  1.04 us

profile of v3, /device:TPU:0, one launch (start us, length us, event | category | flops | bytes accessed | tf_op | source)
XLA Modules:
  0.0 24.5 jit_solution(3211044800283048266)
XLA Ops:
  0.6 22.8 %shard_map.121 = (f32[2,16,32,128]{3,2,1,0:T(8,128)S(1)}, f32[16,32,128]{2,1,0:T(8,128)S(1)}, f32[64,256]{1,0:T(8,128)S(1)}) custom-call(f32[32,16,128]{2,1,0:T(8,128)} %warm_hbm.1, f32[32,16,128]{2,1,0:T(8,128)} %humid_hbm.1, f32[1,64]{1,0:T(1,128)} %bitcast.9, f32[1,64]{1,0:T(1,128)} %bitcast.10, f32[1,112]{1,0:T(1,128)} %bitcast.11, f32[1,112]{1,0:T(1,128)} %bitcast.12, ...), custom_call_target="tpu_custom_call" | custom-call | tf_op jit(solution)/shard_map/pallas_call | solution.py:742
  23.4 1.0 %shard_map.122 = (f32[32,16,128]{2,1,0:T(8,128)}, f32[32,16,128]{2,1,0:T(8,128)}, f32[64,256]{1,0:T(8,128)}) custom-call(f32[2,16,32,128]{3,2,1,0:T(8,128)S(1)} %get-tuple-element.9.res, f32[16,32,128]{2,1,0:T(8,128)S(1)} %get-tuple-element.10.heat, f32[64,256]{1,0:T(8,128)S(1)} %get-tuple-element.11.r_in), custom_call_target="tpu_custom_call" | custom-call | tf_op jit(solution)/shard_map/pallas_call | solution.py:791

commit v4 on v3

--- a/solution.py
+++ b/solution.py
@@ -394,7 +394,7 @@
     return t, m, rates.T
 
 
-CHUNK = 4
+CHUNKS = ((0, 4), (4, 7), (7, 8))
 PAD = 8
 
 
@@ -403,8 +403,8 @@
     warm_hbm, humid_hbm, cx_hbm, cy_hbm, gas_hbm, drop_hbm, sw_hbm, lw_hbm, flags_hbm, slot_hbm,
     res, heat_out, rates_out,
     fields, small, gpoint, flags_ref, slot_ref,
-    loc, buf0, buf1, fin, adv, lines, qt, packed, rad, coef, cloudy, absorber, theta, passed, rates, heat, ucols, corner_send, corner_recv,
-    in_sem, pair_sem, lev_sem, row_send_sem, row_recv_sem, corner_sem, misc_sem,
+    loc, buf0, buf1, fin, got, warm, adv, lines, qt, packed, rad, coef, cloudy, absorber, theta, passed, rates, heat, ucols, ends_send, ends_recv, corner_send, corner_recv,
+    in_sem, pair_sem, lev_sem, row_send_sem, row_recv_sem, corner_sem, misc_sem, gate,
 ):
     g = lax.axis_index("grp")
     x = lax.axis_index("gx")
@@ -415,21 +415,18 @@
     LE = L + M
     RE = R + 2 * M
     RI = R // 2
-    NC = M // CHUNK
     bufs = (buf0, buf1)
 
     sub = lax.broadcasted_iota(jnp.int32, (M, C), 0)
     barrier = pltpu.get_barrier_semaphore()
     partners = [(g, x, oy), (og, x, 0), (og, x, 1)]
-    for gg in (g, og):
-        for xx in (xn, xp):
-            for yy in range(2):
-                partners.append((gg, xx, yy))
+    beside = [(g, xx, yy) for xx in (xn, xp) for yy in range(2)]
+    partners += beside
     for dev in partners:
         pl.semaphore_signal(barrier, inc=1, device_id=dev, device_id_type=MESH)
 
     loads = []
-    pairs = [(slot_hbm, slot_ref), (warm_hbm, fields.at[0]), (humid_hbm, fields.at[1])]
+    pairs = [(warm_hbm, fields.at[0]), (humid_hbm, fields.at[1]), (slot_hbm, slot_ref)]
     pairs += [(cx_hbm, small.at[0]), (cy_hbm, small.at[1])]
     pairs += [(r, gpoint.at[q]) for q, r in enumerate((gas_hbm, drop_hbm, sw_hbm, lw_hbm))]
     pairs += [(flags_hbm, flags_ref)]
@@ -462,92 +459,104 @@
             b[h, :, 0:PAD, :] = edge
             b[h, :, PAD + LE : PAD + LE + 8, :] = edge
 
-    loads[0].wait()
-    half = slot_ref.shape[1]
-    slots = slot_ref[...]
-    rep = (
-        lax.broadcasted_iota(jnp.int32, (half, C), 1) // 2
-        == lax.broadcasted_iota(jnp.int32, (half, C), 0)
-    ).astype(F32).astype(BF)
-    s_hi = (slots // 16).astype(F32).astype(BF)
-    s_lo = (slots % 16).astype(F32).astype(BF)
-    slot_rep = (
-        16.0 * jnp.dot(s_hi, rep, preferred_element_type=F32)
-        + jnp.dot(s_lo, rep, preferred_element_type=F32)
-    ).astype(jnp.int32)
-    s_iota = lax.broadcasted_iota(jnp.int32, (S, C), 0)
-    for i in range(RI):
-        qt[:, i * C : (i + 1) * C] = jnp.where(s_iota == slot_rep[i : i + 1, :], 1.0, 0.0).astype(BF)
-    for n in range(1, 3):
+    for n in range(2):
         loads[n].wait()
     for f in range(2):
         flat = fields.at[f].reshape(L * R, C)
         for r in range(R):
             loc[f, r] = flat[pl.ds(r, L, stride=R), :]
 
-    pl.semaphore_wait(barrier, 11)
-
     own_dst = pl.multiple_of(PAD + M * g, 8)
     lev_src = pl.multiple_of((L - M) * og, 8)
     lev_own = pl.multiple_of(PAD + M * g + (L - M) * og, 8)
     lev_dst = pl.multiple_of(PAD + L * g, 8)
     lev_in = pl.multiple_of(PAD + L * og, 8)
 
-    lead = jnp.where(x == n_gx - 1, 0, 1)
-    for turn in range(2):
-        side = lead if turn == 0 else 1 - lead
-        up = side == 0
-        xx = jnp.where(up, xn, xp)
-        for c in range(NC):
-            d1, d0 = CHUNK * c, CHUNK * (c + 1)
-            s0 = jnp.where(up, R - d0, d1)
-            t0 = jnp.where(up, M - d0, M + R + d1)
-            for f in range(2):
+    def send_levels(r0, r1):
+        for f in range(2):
+            remote(
+                loc.at[f, r0:r1, pl.ds(lev_src, M), :], buf0.at[y, M + r0 : M + r1, pl.ds(lev_dst, M), :],
+                lev_sem.at[0], lev_sem.at[1], (og, x, f),
+            )
+
+    def greet():
+        pl.semaphore_wait(barrier, 7)
+        for dev in beside:
+            pl.semaphore_signal(gate, inc=1, device_id=dev, device_id_type=MESH)
+        for c, (d1, d0) in enumerate(CHUNKS):
+            for side, xx in ((0, xn), (1, xp)):
+                s0 = R - d0 if side == 0 else d1
+                t0 = M - d0 if side == 0 else M + R + d1
+                for f in range(2):
+                    remote(
+                        loc.at[f, s0 : s0 + d0 - d1], buf0.at[y, t0 : t0 + d0 - d1, pl.ds(own_dst, L), :],
+                        row_send_sem.at[0], row_recv_sem.at[side, c], (g, xx, f),
+                    )
+        remote(
+            loc.at[oy], buf0.at[y, M : M + R, pl.ds(own_dst, L), :], pair_sem.at[0], pair_sem.at[1], (g, x, oy)
+        )
+
+    def gather():
+        loads[2].wait()
+        half = slot_ref.shape[1]
+        slots = slot_ref[...]
+        rep = (
+            lax.broadcasted_iota(jnp.int32, (half, C), 1) // 2
+            == lax.broadcasted_iota(jnp.int32, (half, C), 0)
+        ).astype(F32).astype(BF)
+        s_hi = (slots // 16).astype(F32).astype(BF)
+        s_lo = (slots % 16).astype(F32).astype(BF)
+        slot_rep = (
+            16.0 * jnp.dot(s_hi, rep, preferred_element_type=F32)
+            + jnp.dot(s_lo, rep, preferred_element_type=F32)
+        ).astype(jnp.int32)
+        s_iota = lax.broadcasted_iota(jnp.int32, (S, C), 0)
+        for i in range(RI):
+            qt[:, i * C : (i + 1) * C] = jnp.where(s_iota == slot_rep[i : i + 1, :], 1.0, 0.0).astype(BF)
+        parts = []
+        for i in range(RI):
+            col = [loc[f, 2 * i] + loc[f, 2 * i + 1] for f in range(2)]
+            hi, lo = split_bf16(0.25 * jnp.concatenate(col, axis=0))
+            parts.append(jnp.concatenate([hi, lo], axis=0))
+        lhs = jnp.concatenate(parts, axis=1)
+        both = lax.dot_general(
+            lhs, qt[...], (((1,), (1,)), ((), ())), preferred_element_type=F32
+        )
+        both = both[: 2 * L] + both[2 * L :]
+        for h in range(2):
+            packed[h] = both[:, h * B : (h + 1) * B]
+
+    early = jnp.where(x == 0, 1, 1 - g)
+
+    @pl.loop(0, 2)
+    def _(turn):
+        pl.when(turn == 1 - early)(gather)
+        pl.when(turn == early)(greet)
+
+    c_packed = remote(packed.at[og], rad.at[g], misc_sem.at[0], misc_sem.at[1], (og, x, y))
+    send_levels(0, R)
+    def send_corners():
+        for f in range(2):
+            for side in range(2):
+                for j in range(M // 2):
+                    d = j + 1
+                    near, far = (R - d, R - M + d) if side == 0 else (d - 1, M - d - 1)
+                    a = loc[f, near, pl.ds(lev_src, M), :]
+                    b = loc[f, far, pl.ds(lev_src, M), :]
+                    above = jnp.where(sub >= d, a, pltpu.roll(b, d, 0))
+                    below = jnp.where(sub < M - d, a, pltpu.roll(b, M - d, 0))
+                    corner_send[f, side, j] = jnp.where(g == 0, above, below)
+        pl.semaphore_wait(gate, 4)
+        for f in range(2):
+            for side, xx in ((0, xn), (1, xp)):
                 remote(
-                    loc.at[f, pl.ds(s0, CHUNK)], buf0.at[y, pl.ds(t0, CHUNK), pl.ds(own_dst, L), :],
-                    row_send_sem.at[0], row_recv_sem.at[c], (g, xx, f),
+                    corner_send.at[f, side], corner_recv.at[y, side],
+                    corner_sem.at[0], corner_sem.at[1], (og, xx, f),
                 )
 
-    remote(
-        loc.at[oy], buf0.at[y, M : M + R, pl.ds(own_dst, L), :], pair_sem.at[0], pair_sem.at[1], (g, x, oy)
-    )
-    parts = []
-    for i in range(RI):
-        col = [loc[f, 2 * i] + loc[f, 2 * i + 1] for f in range(2)]
-        hi, lo = split_bf16(0.25 * jnp.concatenate(col, axis=0))
-        parts.append(jnp.concatenate([hi, lo], axis=0))
-    lhs = jnp.concatenate(parts, axis=1)
-    both = lax.dot_general(
-        lhs, qt[...], (((1,), (1,)), ((), ())), preferred_element_type=F32
-    )
-    both = both[: 2 * L] + both[2 * L :]
-    for h in range(2):
-        packed[h] = both[:, h * B : (h + 1) * B]
-    c_packed = remote(packed.at[og], rad.at[g], misc_sem.at[0], misc_sem.at[1], (og, x, y))
-    for f in range(2):
-        for side in range(2):
-            for j in range(M // 2):
-                d = j + 1
-                near, far = (R - d, R - M + d) if side == 0 else (d - 1, M - d - 1)
-                a = loc[f, near, pl.ds(lev_src, M), :]
-                b = loc[f, far, pl.ds(lev_src, M), :]
-                above = jnp.where(sub >= d, a, pltpu.roll(b, d, 0))
-                below = jnp.where(sub < M - d, a, pltpu.roll(b, M - d, 0))
-                corner_send[f, side, j] = jnp.where(g == 0, above, below)
-    for f in range(2):
-        for side, xx in ((0, xn), (1, xp)):
-            remote(
-                corner_send.at[f, side], corner_recv.at[y, side],
-                corner_sem.at[0], corner_sem.at[1], (og, xx, f),
-            )
-    for f in range(2):
-        remote(
-            loc.at[f, :, pl.ds(lev_src, M), :], buf0.at[y, M : M + R, pl.ds(lev_dst, M), :],
-            lev_sem.at[0], lev_sem.at[1], (og, x, f),
-        )
-
-    def rows_arrived(c):
-        arrived(buf0.at[:, 0 : 2 * CHUNK, pl.ds(own_dst, L), :], row_recv_sem.at[c])
+    def rows_arrived(side, c):
+        d1, d0 = CHUNKS[c]
+        arrived(buf0.at[:, 0 : d0 - d1, pl.ds(own_dst, L), :], row_recv_sem.at[side, c])
 
     def corners_arrived():
         arrived(corner_recv, corner_sem.at[1])
@@ -586,6 +595,7 @@
         src_ref=rates.at[og], dst_ref=heat.at[g], send_sem=misc_sem.at[2], recv_sem=misc_sem.at[3],
         device_id=(og, x, y), device_id_type=MESH,
     )
+    pl.when(g == 1)(send_corners)
     for o in range(2):
         @pl.when(og == o)
         def _():
@@ -627,20 +637,22 @@
         @pl.when(og == o)
         def _():
             c_heat.start()
+        if o == 0:
+            pl.when(g == 0)(send_corners)
     heat[g] = rates[g]
 
     def stencil(k, i0, n):
         src, dst = bufs[(k - 1) % 2], bufs[k % 2]
         lane = lax.broadcasted_iota(jnp.int32, (n * LE, C), 1)
-        span = [src[h, i0 - 1 : i0 + n + 1, PAD : PAD + LE, :] for h in range(2)]
+        span = [src[h, pl.ds(i0 - 1, n + 2), PAD : PAD + LE, :] for h in range(2)]
         mid = [v[1 : n + 1].reshape(n * LE, C) for v in span]
         right = [pltpu.roll(v, 1, 1) for v in mid]
         left = [pltpu.roll(v, C - 1, 1) for v in mid]
         for h in range(2):
             prev = jnp.where(lane == 0, right[1 - h], right[h]).reshape(n, LE, C)
             nxt = jnp.where(lane == C - 1, left[1 - h], left[h]).reshape(n, LE, C)
-            up = src[h, i0 : i0 + n, PAD - 1 : PAD + LE - 1, :]
-            down = src[h, i0 : i0 + n, PAD + 1 : PAD + LE + 1, :]
+            up = src[h, pl.ds(i0, n), PAD - 1 : PAD + LE - 1, :]
+            down = src[h, pl.ds(i0, n), PAD + 1 : PAD + LE + 1, :]
             new = (
                 (1.0 - 4.0 * NU_H - 2.0 * NU_V) * span[h][1 : n + 1]
                 + NU_V * (up + down)
@@ -650,15 +662,25 @@
                 + adv[3][None] * prev
             )
             if k == SWEEPS:
-                fin[h, i0 - M : i0 - M + n] = new
+                fin[h, pl.ds(i0 - M, n)] = new
             else:
-                dst[h, i0 : i0 + n, PAD : PAD + LE, :] = new
-
-    def strip(c):
-        h = CHUNK * (c + 1)
+                dst[h, pl.ds(i0, n), PAD : PAD + LE, :] = new
+
+    mine = pl.multiple_of(M * g, 8)
+
+    def widen(*parts, last=3):
         for k in range(1, SWEEPS + 1):
-            stencil(k, M + k - h, CHUNK)
-            stencil(k, M + R - (k - h) - CHUNK, CHUNK)
+            for side, d1, d0 in parts:
+                for e in range(d0, d1, -2):
+                    n = min(2, e - d1)
+                    stencil(k, M + k - e if side == 0 else M + R - k + e - n, n)
+        for side, d1, d0 in parts:
+            n = d0 - d1
+            r = SWEEPS - d0 if side == 0 else R - SWEEPS + d1
+            remote(
+                fin.at[oy, r : r + n, pl.ds(mine, L), :], got.at[r : r + n],
+                pair_sem.at[2], pair_sem.at[last], (g, x, oy),
+            )
 
     arrived(buf0.at[oy, M : M + R, pl.ds(own_dst, L), :], pair_sem.at[1])
     arrived(buf0.at[:, M : M + R, pl.ds(lev_in, M), :], lev_sem.at[1])
@@ -669,62 +691,108 @@
             stencil(k, i0, n)
             i0 += n
 
+    LH = L // 2
+    lane = lax.broadcasted_iota(jnp.int32, (LH, C), 1)
+    even = lane % 2 == 0
+
     c_heat.wait()
     hi, lo = split_bf16(jnp.concatenate([heat[h, hb] for h in range(2) for hb in range(B // 128)], axis=1))
     spread = jnp.dot(jnp.concatenate([hi, lo], axis=0), qt[...], preferred_element_type=F32)
     spread = spread[:L] + spread[L:]
     for i in range(RI):
         ucols[y, 1 + i] = spread[:, i * C : (i + 1) * C]
-    for i, t, xx in ((1, RI + 1, xp), (RI, 0, xn)):
+    for e, i in ((1, 0), (0, RI - 1)):
+        v = spread[:, i * C : (i + 1) * C]
+        ends_send[e] = jnp.where(even, v[:LH], v[LH:])
+    for e, xx in ((1, xp), (0, xn)):
         for yy in range(2):
-            remote(ucols.at[y, i], ucols.at[y, t], misc_sem.at[4], misc_sem.at[5], (g, xx, yy))
-    c_cols = remote(
+            remote(ends_send.at[e], ends_recv.at[y, e], misc_sem.at[4], misc_sem.at[5], (g, xx, yy))
+    remote(
         ucols.at[y, 1 : RI + 1], ucols.at[y, 1 : RI + 1], misc_sem.at[6], misc_sem.at[7], (g, x, oy)
     )
-
-    mine = pl.multiple_of(M * g, 8)
     corners_arrived()
-    for c in range(NC):
-        rows_arrived(c)
-        strip(c)
-        h = CHUNK * (c + 1)
-        for r in (M - h, R - M + h - CHUNK):
-            remote(
-                fin.at[oy, r : r + CHUNK, pl.ds(mine, L), :], res.at[y, r : r + CHUNK],
-                pair_sem.at[2], pair_sem.at[3], (g, x, oy),
-            )
-    res[y] = fin[y, :, pl.ds(mine, L), :]
-
-    c_cols.wait()
-    arrived(ucols.at[:, 0:2], misc_sem.at[5])
-    lane = lax.broadcasted_iota(jnp.int32, (L, C), 1)
-    even = lane % 2 == 0
-    cols = []
-    for i in range(RI + 2):
-        v, o = ucols[y, i], ucols[oy, i]
-        prev = jnp.where(lane == 0, pltpu.roll(o, 1, 1), pltpu.roll(v, 1, 1))
-        nxt = jnp.where(lane == C - 1, pltpu.roll(o, C - 1, 1), pltpu.roll(v, C - 1, 1))
-        cols.append(HEATING_INTERVAL * (0.75 * v + 0.25 * jnp.where(even, prev, nxt)))
-    for i in range(RI):
-        heat_out[2 * i] = 0.75 * cols[i + 1] + 0.25 * cols[i]
-        heat_out[2 * i + 1] = 0.75 * cols[i + 1] + 0.25 * cols[i + 2]
+
+    def heat_rows():
+        left(ucols.at[y, 1 : RI + 1], misc_sem.at[6])
+        arrived(ucols.at[oy, 1 : RI + 1], misc_sem.at[7])
+        arrived(ends_recv, misc_sem.at[5])
+        for h in range(2):
+            for e, i in ((0, 0), (1, RI + 1)):
+                v = ends_recv[h, e]
+                ucols[h, i, 0:LH] = jnp.where(even, v, pltpu.roll(v, 1, 1))
+                ucols[h, i, LH:L] = jnp.where(even, pltpu.roll(v, C - 1, 1), v)
+        lane = lax.broadcasted_iota(jnp.int32, (L, C), 1)
+        cols = []
+        for i in range(RI + 2):
+            v, o = ucols[y, i], ucols[oy, i]
+            prev = jnp.where(lane == 0, pltpu.roll(o, 1, 1), pltpu.roll(v, 1, 1))
+            nxt = jnp.where(lane == C - 1, pltpu.roll(o, C - 1, 1), pltpu.roll(v, C - 1, 1))
+            cols.append(HEATING_INTERVAL * (0.75 * v + 0.25 * jnp.where(lane % 2 == 0, prev, nxt)))
+        for i in range(RI):
+            warm[2 * i] = 0.75 * cols[i + 1] + 0.25 * cols[i]
+            warm[2 * i + 1] = 0.75 * cols[i + 1] + 0.25 * cols[i + 2]
+
+    def rows_in(first):
+        second = 1 - first
+        rows_arrived(first, 0)
+        widen((first, 0, 4))
+        rows_arrived(first, 1)
+        rows_arrived(first, 2)
+        rows_arrived(second, 0)
+        widen((first, 4, 8), (second, 0, 4))
+        rows_arrived(second, 1)
+        widen((second,) + CHUNKS[1], last=4)
+        heat_rows()
+        rows_arrived(second, 2)
+        widen((second,) + CHUNKS[2], last=4)
+
+    for first in range(2):
+        pl.when(lax.rem(x, 2) == first)(functools.partial(rows_in, first))
+    flat = res.reshape(2 * L * R, C)
+    heat_flat = heat_out.reshape(L * R, C)
+    for r in range(R):
+        flat[pl.ds(y * (L * R) + r, L, stride=R), :] = fin[y, r, pl.ds(mine, L), :]
+        heat_flat[pl.ds(r, L, stride=R), :] = warm[r]
+    late = M - CHUNKS[0][1]
+    arrived(got.at[0 : R - late], pair_sem.at[3])
+
+    def take(side, near, far):
+        for e in range(near + 1, far + 1):
+            r = M - e if side == 0 else R - M + e - 1
+            flat[pl.ds(oy * (L * R) + r, L, stride=R), :] = got[r]
+
+    def take_early(first):
+        take(first, 0, M)
+        take(1 - first, 0, M - late)
+
+    def take_late(first):
+        take(1 - first, M - late, M)
+
+    for first in range(2):
+        pl.when(lax.rem(x, 2) == first)(functools.partial(take_early, first))
     left(buf0.at[:, 0 : 2 * M, 0:L, :], row_send_sem.at[0])
     left(corner_send, corner_sem.at[0])
     left(buf0.at[:, 0:R, 0:M, :], lev_sem.at[0])
     left(loc.at[oy], pair_sem.at[0])
-    left(ucols.at[:, 0:2], misc_sem.at[4])
-    left(res.at[oy], pair_sem.at[2])
-    arrived(res.at[oy], pair_sem.at[3])
-
-
-def settle(res, heat, r_in, t_out, m_out, r_out):
-    L, R, C = t_out.shape
-    t_flat = t_out.reshape(L * R, C)
-    m_flat = m_out.reshape(L * R, C)
-    for r in range(R):
-        t_flat[pl.ds(r, L, stride=R), :] = res[0, r] + heat[r]
-        m_flat[pl.ds(r, L, stride=R), :] = res[1, r]
-    r_out[...] = r_in[...]
+    left(ends_recv, misc_sem.at[4])
+    arrived(got.at[0:late], pair_sem.at[4])
+    for first in range(2):
+        pl.when(lax.rem(x, 2) == first)(functools.partial(take_late, first))
+    left(got, pair_sem.at[2])
+
+
+def settle(res, heat, r_in, t_out, m_out, r_out, t_ref, sem):
+    copies = [
+        pltpu.make_async_copy(res.at[1], m_out, sem.at[0]),
+        pltpu.make_async_copy(r_in, r_out, sem.at[1]),
+        pltpu.make_async_copy(t_ref, t_out, sem.at[2]),
+    ]
+    copies[0].start()
+    copies[1].start()
+    t_ref[...] = res[0] + heat[...]
+    copies[2].start()
+    for c in copies:
+        c.wait()
 
 
 def pair_body(n_gx, n_gy, warm, humid, cx, cy, gas, drop, sw, lw, flags, slots):
@@ -736,14 +804,13 @@
     LE = L + M
     LP = PAD + LE + 8
     RE = R + 2 * M
-    NC = M // CHUNK
     vmem = pl.BlockSpec(memory_space=pltpu.VMEM)
     hbm = pl.BlockSpec(memory_space=pltpu.HBM)
     res, heat, rates = pl.pallas_call(
         functools.partial(pair_kernel, n_gx, L, R, C, S, B, G),
         out_shape=(
-            jax.ShapeDtypeStruct((2, R, L, C), F32),
-            jax.ShapeDtypeStruct((R, L, C), F32),
+            jax.ShapeDtypeStruct((2, L, R, C), F32),
+            jax.ShapeDtypeStruct((L, R, C), F32),
             jax.ShapeDtypeStruct((2 * L, B), F32),
         ),
         in_specs=[hbm] * 10,
@@ -758,6 +825,8 @@
             pltpu.VMEM((2, RE, LP, C), F32),
             pltpu.VMEM((2, RE, LP, C), F32),
             pltpu.VMEM((2, R, LE, C), F32),
+            pltpu.VMEM((R, L, C), F32),
+            pltpu.VMEM((R, L, C), F32),
             pltpu.VMEM((4, LE, C), F32),
             pltpu.VMEM((2, 2 * L, C), F32),
             pltpu.VMEM((S, (R // 2) * C), BF),
@@ -771,15 +840,18 @@
             pltpu.VMEM((2, B // 128, L, 128), F32),
             pltpu.VMEM((2, B // 128, L, 128), F32),
             pltpu.VMEM((2, R // 2 + 2, L, C), F32),
+            pltpu.VMEM((2, L // 2, C), F32),
+            pltpu.VMEM((2, 2, L // 2, C), F32),
             pltpu.VMEM((2, 2, M // 2, M, C), F32),
             pltpu.VMEM((2, 2, M // 2, M, C), F32),
             pltpu.SemaphoreType.DMA((10,)),
-            pltpu.SemaphoreType.DMA((4,)),
+            pltpu.SemaphoreType.DMA((5,)),
             pltpu.SemaphoreType.DMA((2,)),
             pltpu.SemaphoreType.DMA((1,)),
-            pltpu.SemaphoreType.DMA((NC,)),
+            pltpu.SemaphoreType.DMA((2, len(CHUNKS))),
             pltpu.SemaphoreType.DMA((2,)),
             pltpu.SemaphoreType.DMA((8,)),
+            pltpu.SemaphoreType.REGULAR,
         ],
         compiler_params=pltpu.CompilerParams(
             collective_id=0, has_side_effects=True, vmem_limit_bytes=32 * 1024 * 1024
@@ -796,7 +868,11 @@
             jax.ShapeDtypeStruct((2 * L, B), F32),
         ),
         in_specs=[vmem] * 3,
-        out_specs=(vmem,) * 3,
+        out_specs=(hbm,) * 3,
+        scratch_shapes=[
+            pltpu.VMEM((L, R, C), F32),
+            pltpu.SemaphoreType.DMA((3,)),
+        ],
         compiler_params=pltpu.CompilerParams(vmem_limit_bytes=8 * 1024 * 1024),
     )(res, heat, rates)
     return t, m, rates.T

time: 24.6 us -> 22.9 us (0.931)
  Pallas kernels: 23.8 us -> 22.1 us
    pallas_call x1, Pallas kernels: 22.8 us -> 21.3 us  [pair_body(): pl.pallas_call(functools.partial(pair_kernel, n_gx, L, R, C, S, B, G), ou...]
where the time goes in v4:
time: 22.9 us; the launch traced here: 22.8 us
  Pallas kernels  22.1 us (97%)
  between operations  0.64 us (3%)
    pallas_call x1, Pallas kernels, pair_body(): pl.pallas_call(functools.partial(pair_kernel, n_gx, L, R, C, S, B, G), ou...  21.3 us
    pallas_call x1, Pallas kernels, pair_body(): pl.pallas_call(settle, out_shape=(jax.ShapeDtypeStruct((L, R, C), F32), j...  0.84 us

profile of v4, /device:TPU:0, one launch (start us, length us, event | category | flops | bytes accessed | tf_op | source)
XLA Modules:
  0.0 22.8 jit_solution(12615225431311623465)
XLA Ops:
  0.6 21.3 %shard_map.121 = (f32[2,32,16,128]{3,2,1,0:T(8,128)S(1)}, f32[32,16,128]{2,1,0:T(8,128)S(1)}, f32[64,256]{1,0:T(8,128)S(1)}) custom-call(f32[32,16,128]{2,1,0:T(8,128)} %warm_hbm.1, f32[32,16,128]{2,1,0:T(8,128)} %humid_hbm.1, f32[1,64]{1,0:T(1,128)} %bitcast.9, f32[1,64]{1,0:T(1,128)} %bitcast.10, f32[1,112]{1,0:T(1,128)} %bitcast.11, f32[1,112]{1,0:T(1,128)} %bitcast.12, ...), custom_call_target="tpu_custom_call" | custom-call | tf_op jit(solution)/shard_map/pallas_call | solution.py:809
  22.0 0.8 %shard_map.122 = (f32[32,16,128]{2,1,0:T(8,128)}, f32[32,16,128]{2,1,0:T(8,128)}, f32[64,256]{1,0:T(8,128)}) custom-call(f32[2,32,16,128]{3,2,1,0:T(8,128)S(1)} %get-tuple-element.9.res, f32[32,16,128]{2,1,0:T(8,128)S(1)} %get-tuple-element.10.heat, f32[64,256]{1,0:T(8,128)S(1)} %get-tuple-element.11.r_in), custom_call_target="tpu_custom_call" | custom-call | tf_op jit(solution)/shard_map/pallas_call | solution.py:863

commit v5 on v4

--- a/solution.py
+++ b/solution.py
@@ -403,7 +403,7 @@
     warm_hbm, humid_hbm, cx_hbm, cy_hbm, gas_hbm, drop_hbm, sw_hbm, lw_hbm, flags_hbm, slot_hbm,
     res, heat_out, rates_out,
     fields, small, gpoint, flags_ref, slot_ref,
-    loc, buf0, buf1, fin, got, warm, adv, lines, qt, packed, rad, coef, cloudy, absorber, theta, passed, rates, heat, ucols, ends_send, ends_recv, corner_send, corner_recv,
+    loc, buf0, buf1, fin, got, adv, lines, qt, packed, rad, coef, cloudy, absorber, theta, passed, rates, heat, ucols, ends_send, ends_recv, corner_send, corner_recv,
     in_sem, pair_sem, lev_sem, row_send_sem, row_recv_sem, corner_sem, misc_sem, gate,
 ):
     g = lax.axis_index("grp")
@@ -425,6 +425,13 @@
     for dev in partners:
         pl.semaphore_signal(barrier, inc=1, device_id=dev, device_id_type=MESH)
 
+    tail = x == n_gx - 1
+
+    @pl.when(x == 0)
+    def _():
+        for yy in range(2):
+            pl.semaphore_signal(barrier, inc=1, device_id=(og, xp, yy), device_id_type=MESH)
+
     loads = []
     pairs = [(warm_hbm, fields.at[0]), (humid_hbm, fields.at[1]), (slot_hbm, slot_ref)]
     pairs += [(cx_hbm, small.at[0]), (cy_hbm, small.at[1])]
@@ -480,9 +487,15 @@
             )
 
     def greet():
-        pl.semaphore_wait(barrier, 7)
-        for dev in beside:
-            pl.semaphore_signal(gate, inc=1, device_id=dev, device_id_type=MESH)
+        pl.semaphore_wait(barrier, jnp.where(tail, 9, 7))
+
+        def pass_on(xx):
+            for yy in range(2):
+                pl.semaphore_signal(gate, inc=1, device_id=(g, xx, yy), device_id_type=MESH)
+
+        pass_on(xn)
+        pl.when(x > 0)(functools.partial(pass_on, xp))
+
         for c, (d1, d0) in enumerate(CHUNKS):
             for side, xx in ((0, xn), (1, xp)):
                 s0 = R - d0 if side == 0 else d1
@@ -525,8 +538,21 @@
         both = both[: 2 * L] + both[2 * L :]
         for h in range(2):
             packed[h] = both[:, h * B : (h + 1) * B]
-
-    early = jnp.where(x == 0, 1, 1 - g)
+        for n in range(3, len(loads)):
+            loads[n].wait()
+        for q in range(2):
+            lines[q] = jnp.broadcast_to(small[q], (C, 2 * L)).T
+        for q in range(2):
+            part = 0.5 * lines[q, pl.ds(pl.multiple_of((L - M) * g, 8), LE), :]
+            adv[2 * q] = NU_H - part
+            adv[2 * q + 1] = NU_H + part
+        log2e = 1.0 / math.log(2.0)
+        for q, scale in enumerate((-log2e, -log2e, 1.0, 1.0)):
+            coef[q] = jnp.broadcast_to(gpoint[q] * scale, (128, G)).T
+        for hb in range(B // 128):
+            cloudy[hb] = flags_ref[:, hb * 128 : (hb + 1) * 128].astype(F32)
+
+    early = jnp.where(x == 0, 1, 0)
 
     @pl.loop(0, 2)
     def _(turn):
@@ -534,25 +560,31 @@
         pl.when(turn == early)(greet)
 
     c_packed = remote(packed.at[og], rad.at[g], misc_sem.at[0], misc_sem.at[1], (og, x, y))
+    for f in range(2):
+        for side in range(2):
+            for j in range(M // 2):
+                d = j + 1
+                near, far = (R - d, R - M + d) if side == 0 else (d - 1, M - d - 1)
+                a = loc[f, near, pl.ds(lev_src, M), :]
+                b = loc[f, far, pl.ds(lev_src, M), :]
+                above = jnp.where(sub >= d, a, pltpu.roll(b, d, 0))
+                below = jnp.where(sub < M - d, a, pltpu.roll(b, M - d, 0))
+                corner_send[f, side, j] = jnp.where(g == 0, above, below)
+
+    def corners_to(side, xx):
+        for f in range(2):
+            remote(
+                corner_send.at[f, side], corner_recv.at[y, side],
+                corner_sem.at[0], corner_sem.at[1], (og, xx, f),
+            )
+
+    def send_corners():
+        pl.semaphore_wait(gate, jnp.where(tail, 2, 4))
+        pl.when(x < n_gx - 1)(functools.partial(corners_to, 0, xn))
+        corners_to(1, xp)
+
+    pl.when(tail)(functools.partial(corners_to, 0, xn))
     send_levels(0, R)
-    def send_corners():
-        for f in range(2):
-            for side in range(2):
-                for j in range(M // 2):
-                    d = j + 1
-                    near, far = (R - d, R - M + d) if side == 0 else (d - 1, M - d - 1)
-                    a = loc[f, near, pl.ds(lev_src, M), :]
-                    b = loc[f, far, pl.ds(lev_src, M), :]
-                    above = jnp.where(sub >= d, a, pltpu.roll(b, d, 0))
-                    below = jnp.where(sub < M - d, a, pltpu.roll(b, M - d, 0))
-                    corner_send[f, side, j] = jnp.where(g == 0, above, below)
-        pl.semaphore_wait(gate, 4)
-        for f in range(2):
-            for side, xx in ((0, xn), (1, xp)):
-                remote(
-                    corner_send.at[f, side], corner_recv.at[y, side],
-                    corner_sem.at[0], corner_sem.at[1], (og, xx, f),
-                )
 
     def rows_arrived(side, c):
         d1, d0 = CHUNKS[c]
@@ -573,20 +605,6 @@
 
     rad[g] = packed[g]
     buf0[y, M : M + R, pl.ds(own_dst, L), :] = loc[y]
-
-    for n in range(3, len(loads)):
-        loads[n].wait()
-    for q in range(2):
-        lines[q] = jnp.broadcast_to(small[q], (C, 2 * L)).T
-    for q in range(2):
-        part = 0.5 * lines[q, pl.ds(pl.multiple_of((L - M) * g, 8), LE), :]
-        adv[2 * q] = NU_H - part
-        adv[2 * q + 1] = NU_H + part
-    log2e = 1.0 / math.log(2.0)
-    for q, scale in enumerate((-log2e, -log2e, 1.0, 1.0)):
-        coef[q] = jnp.broadcast_to(gpoint[q] * scale, (128, G)).T
-    for hb in range(B // 128):
-        cloudy[hb] = flags_ref[:, hb * 128 : (hb + 1) * 128].astype(F32)
 
     GB = G // 8
     HB = B // 128
@@ -669,11 +687,12 @@
     mine = pl.multiple_of(M * g, 8)
 
     def widen(*parts, last=3):
-        for k in range(1, SWEEPS + 1):
-            for side, d1, d0 in parts:
-                for e in range(d0, d1, -2):
-                    n = min(2, e - d1)
-                    stencil(k, M + k - e if side == 0 else M + R - k + e - n, n)
+        for d in range(max(d0 - d1 for _, d1, d0 in parts)):
+            for k in range(1, SWEEPS + 1):
+                for side, d1, d0 in parts:
+                    e = d1 + d + 1
+                    if e <= d0:
+                        stencil(k, M + k - e if side == 0 else M + R - 1 - k + e, 1)
         for side, d1, d0 in parts:
             n = d0 - d1
             r = SWEEPS - d0 if side == 0 else R - SWEEPS + d1
@@ -711,6 +730,8 @@
         ucols.at[y, 1 : RI + 1], ucols.at[y, 1 : RI + 1], misc_sem.at[6], misc_sem.at[7], (g, x, oy)
     )
     corners_arrived()
+
+    heat_flat = heat_out.reshape(L * R, C)
 
     def heat_rows():
         left(ucols.at[y, 1 : RI + 1], misc_sem.at[6])
@@ -729,8 +750,8 @@
             nxt = jnp.where(lane == C - 1, pltpu.roll(o, C - 1, 1), pltpu.roll(v, C - 1, 1))
             cols.append(HEATING_INTERVAL * (0.75 * v + 0.25 * jnp.where(lane % 2 == 0, prev, nxt)))
         for i in range(RI):
-            warm[2 * i] = 0.75 * cols[i + 1] + 0.25 * cols[i]
-            warm[2 * i + 1] = 0.75 * cols[i + 1] + 0.25 * cols[i + 2]
+            heat_flat[pl.ds(2 * i, L, stride=R), :] = 0.75 * cols[i + 1] + 0.25 * cols[i]
+            heat_flat[pl.ds(2 * i + 1, L, stride=R), :] = 0.75 * cols[i + 1] + 0.25 * cols[i + 2]
 
     def rows_in(first):
         second = 1 - first
@@ -742,17 +763,14 @@
         widen((first, 4, 8), (second, 0, 4))
         rows_arrived(second, 1)
         widen((second,) + CHUNKS[1], last=4)
-        heat_rows()
         rows_arrived(second, 2)
         widen((second,) + CHUNKS[2], last=4)
 
     for first in range(2):
         pl.when(lax.rem(x, 2) == first)(functools.partial(rows_in, first))
     flat = res.reshape(2 * L * R, C)
-    heat_flat = heat_out.reshape(L * R, C)
     for r in range(R):
         flat[pl.ds(y * (L * R) + r, L, stride=R), :] = fin[y, r, pl.ds(mine, L), :]
-        heat_flat[pl.ds(r, L, stride=R), :] = warm[r]
     late = M - CHUNKS[0][1]
     arrived(got.at[0 : R - late], pair_sem.at[3])
 
@@ -770,6 +788,7 @@
 
     for first in range(2):
         pl.when(lax.rem(x, 2) == first)(functools.partial(take_early, first))
+    heat_rows()
     left(buf0.at[:, 0 : 2 * M, 0:L, :], row_send_sem.at[0])
     left(corner_send, corner_sem.at[0])
     left(buf0.at[:, 0:R, 0:M, :], lev_sem.at[0])
@@ -825,7 +844,6 @@
             pltpu.VMEM((2, RE, LP, C), F32),
             pltpu.VMEM((2, RE, LP, C), F32),
             pltpu.VMEM((2, R, LE, C), F32),
-            pltpu.VMEM((R, L, C), F32),
             pltpu.VMEM((R, L, C), F32),
             pltpu.VMEM((4, LE, C), F32),
             pltpu.VMEM((2, 2 * L, C), F32),

time: 22.9 us -> 21.8 us (0.952)
  Pallas kernels: 22.1 us -> 21 us
    pallas_call x1, Pallas kernels: 21.3 us -> 20.2 us  [pair_body(): pl.pallas_call(functools.partial(pair_kernel, n_gx, L, R, C, S, B, G), ou...]
where the time goes in v5:
time: 21.8 us; the launch traced here: 21.6 us
  Pallas kernels  21 us (96%)
  between operations  0.64 us (3%)
    pallas_call x1, Pallas kernels, pair_body(): pl.pallas_call(functools.partial(pair_kernel, n_gx, L, R, C, S, B, G), ou...  20.2 us
    pallas_call x1, Pallas kernels, pair_body(): pl.pallas_call(settle, out_shape=(jax.ShapeDtypeStruct((L, R, C), F32), j...  0.84 us

profile of v5, /device:TPU:0, one launch (start us, length us, event | category | flops | bytes accessed | tf_op | source)
XLA Modules:
  0.0 21.6 jit_solution(3362727331107976026)
XLA Ops:
  0.6 20.2 %shard_map.121 = (f32[2,32,16,128]{3,2,1,0:T(8,128)S(1)}, f32[32,16,128]{2,1,0:T(8,128)S(1)}, f32[64,256]{1,0:T(8,128)S(1)}) custom-call(f32[32,16,128]{2,1,0:T(8,128)} %warm_hbm.1, f32[32,16,128]{2,1,0:T(8,128)} %humid_hbm.1, f32[1,64]{1,0:T(1,128)} %bitcast.9, f32[1,64]{1,0:T(1,128)} %bitcast.10, f32[1,112]{1,0:T(1,128)} %bitcast.11, f32[1,112]{1,0:T(1,128)} %bitcast.12, ...), custom_call_target="tpu_custom_call" | custom-call | tf_op jit(solution)/shard_map/pallas_call | solution.py:828
  20.8 0.8 %shard_map.122 = (f32[32,16,128]{2,1,0:T(8,128)}, f32[32,16,128]{2,1,0:T(8,128)}, f32[64,256]{1,0:T(8,128)}) custom-call(f32[2,32,16,128]{3,2,1,0:T(8,128)S(1)} %get-tuple-element.9.res, f32[32,16,128]{2,1,0:T(8,128)S(1)} %get-tuple-element.10.heat, f32[64,256]{1,0:T(8,128)S(1)} %get-tuple-element.11.r_in), custom_call_target="tpu_custom_call" | custom-call | tf_op jit(solution)/shard_map/pallas_call | solution.py:881

commit v6 on v5

--- a/solution.py
+++ b/solution.py
@@ -404,7 +404,7 @@
     res, heat_out, rates_out,
     fields, small, gpoint, flags_ref, slot_ref,
     loc, buf0, buf1, fin, got, adv, lines, qt, packed, rad, coef, cloudy, absorber, theta, passed, rates, heat, ucols, ends_send, ends_recv, corner_send, corner_recv,
-    in_sem, pair_sem, lev_sem, row_send_sem, row_recv_sem, corner_sem, misc_sem, gate,
+    in_sem, pair_sem, lev_sem, row_send_sem, row_recv_sem, corner_sem, misc_sem, half_sem, gate,
 ):
     g = lax.axis_index("grp")
     x = lax.axis_index("gx")
@@ -559,7 +559,13 @@
         pl.when(turn == 1 - early)(gather)
         pl.when(turn == early)(greet)
 
-    c_packed = remote(packed.at[og], rad.at[g], misc_sem.at[0], misc_sem.at[1], (og, x, y))
+    c_packed = [
+        remote(
+            packed.at[og, :, hb * 128 : (hb + 1) * 128], rad.at[g, :, hb * 128 : (hb + 1) * 128],
+            half_sem.at[0, hb], half_sem.at[1, hb], (og, x, y),
+        )
+        for hb in range(B // 128)
+    ]
     for f in range(2):
         for side in range(2):
             for j in range(M // 2):
@@ -615,16 +621,14 @@
     )
     pl.when(g == 1)(send_corners)
     for o in range(2):
-        @pl.when(og == o)
-        def _():
-            c_packed.wait()
-
-        mo = rad[o, L : 2 * L, :]
-        soft = jnp.maximum(mo, 0.0) + jnp.log1p(jnp.exp(-jnp.abs(mo)))
         for hb in range(HB):
-            absorber[hb, o * L : (o + 1) * L, :] = soft[:, hb * 128 : (hb + 1) * 128]
-            theta[hb, o * L : (o + 1) * L, :] = rad[o, 0:L, hb * 128 : (hb + 1) * 128]
-        for hb in range(HB):
+            pl.when(og == o)(c_packed[hb].wait)
+            cut = slice(hb * 128, (hb + 1) * 128)
+            mo = rad[o, L : 2 * L, cut]
+            soft = jnp.maximum(mo, 0.0) + jnp.log1p(jnp.exp(-jnp.abs(mo)))
+            absorber[hb, o * L : (o + 1) * L, :] = soft
+            theta[hb, o * L : (o + 1) * L, :] = rad[o, 0:L, cut]
+
             def level(l, flux, o=o, hb=hb):
                 lg = l + o * L
                 a = jnp.broadcast_to(absorber[hb, pl.ds(lg, 1), :], (8, 128))
@@ -869,6 +873,7 @@
             pltpu.SemaphoreType.DMA((2, len(CHUNKS))),
             pltpu.SemaphoreType.DMA((2,)),
             pltpu.SemaphoreType.DMA((8,)),
+            pltpu.SemaphoreType.DMA((2, B // 128)),
             pltpu.SemaphoreType.REGULAR,
         ],
         compiler_params=pltpu.CompilerParams(

time: 21.8 us -> 21.7 us (level)
  no operation moved by 1% of the time
where the time goes in v6:
time: 21.7 us; the launch traced here: 21.5 us
  Pallas kernels  20.9 us (96%)
  between operations  0.64 us (3%)
    pallas_call x1, Pallas kernels, pair_body(): pl.pallas_call(functools.partial(pair_kernel, n_gx, L, R, C, S, B, G), ou...  20.1 us
    pallas_call x1, Pallas kernels, pair_body(): pl.pallas_call(settle, out_shape=(jax.ShapeDtypeStruct((L, R, C), F32), j...  0.84 us

profile of v6, /device:TPU:0, one launch (start us, length us, event | category | flops | bytes accessed | tf_op | source)
XLA Modules:
  0.0 21.5 jit_solution(1000017121016714917)
XLA Ops:
  0.6 20.1 %shard_map.121 = (f32[2,32,16,128]{3,2,1,0:T(8,128)S(1)}, f32[32,16,128]{2,1,0:T(8,128)S(1)}, f32[64,256]{1,0:T(8,128)S(1)}) custom-call(f32[32,16,128]{2,1,0:T(8,128)} %warm_hbm.1, f32[32,16,128]{2,1,0:T(8,128)} %humid_hbm.1, f32[1,64]{1,0:T(1,128)} %bitcast.9, f32[1,64]{1,0:T(1,128)} %bitcast.10, f32[1,112]{1,0:T(1,128)} %bitcast.11, f32[1,112]{1,0:T(1,128)} %bitcast.12, ...), custom_call_target="tpu_custom_call" | custom-call | tf_op jit(solution)/shard_map/pallas_call | solution.py:832
  20.7 0.8 %shard_map.122 = (f32[32,16,128]{2,1,0:T(8,128)}, f32[32,16,128]{2,1,0:T(8,128)}, f32[64,256]{1,0:T(8,128)}) custom-call(f32[2,32,16,128]{3,2,1,0:T(8,128)S(1)} %get-tuple-element.9.res, f32[32,16,128]{2,1,0:T(8,128)S(1)} %get-tuple-element.10.heat, f32[64,256]{1,0:T(8,128)S(1)} %get-tuple-element.11.r_in), custom_call_target="tpu_custom_call" | custom-call | tf_op jit(solution)/shard_map/pallas_call | solution.py:886
